TPU v7x, 256 devices: a whole 4x4x8 slice. The times are simulated.
256 devices in a mesh: xy: 64 (over z_hi, y, x, core), gz: 4 (over z_lo).
Axes of the slice: x: 4, y: 4, z: 8 (z_hi: 2, z_lo: 4; z = z_hi * 4 + z_lo), core: 2. Of those that a mesh axis runs over, the one named last changes fastest.
Arguments:
- field: float32 [64, 2, 3, 512, 256], P('gz', None, None, 'xy'), may hold values from -6 to 6
- source: float32 [64, 2, 3, 512, 256], P('gz', None, None, 'xy'), may hold values from -6 to 6
- classes: int32 [64, 512, 256], P('gz', 'xy'), may hold values from 0 to 15
- boundary: int32 [64, 512, 256], P('gz', 'xy'), may hold values 0 or 1
- conductance: float32 [16], replicated, may hold values from 0.001 to 1
- angles: float32 [3], replicated, may hold values from -3.140625 to 3.140625
- strengths: float32 [3], replicated, may hold values from 0.5 to 2
Outputs:
- relaxed: float32 [64, 2, 3, 512, 256], P('gz', None, None, 'xy')
All inputs are finite; a program needn't handle non-finite values. No bound on the sum of `boundary` on one device may be relied on, other than what follows from the above.
Results may differ from a plain program's by a relative error of at most 0.00029.
Values sent between devices are 32-bit elements; how exact they have to be, the bound alone decides.
A program may use at most 64 MiB of HBM per device.

v0:
```python
import functools

import jax
import jax.numpy as jnp
from jax import lax
from jax.experimental import pallas as pl
from jax.experimental.pallas import tpu as pltpu
from jax.sharding import PartitionSpec as P

SWEEPS = 2
PIECES = 2
VMEM_LIMIT = 62 * 2**20

coupling = 0.1
penalty = 4.0


def mul(a, b):
    return (a[0] * b[0] - a[1] * b[1], a[0] * b[1] + a[1] * b[0])


def add(a, b):
    return (a[0] + b[0], a[1] + b[1])


def inv(a):
    weight = 1.0 / (a[0] * a[0] + a[1] * a[1])
    return (a[0] * weight, -a[1] * weight)


def one_minus(a):
    return (1.0 - a[0], -a[1])


def get(ref, *at):
    return (ref[at + (0,)], ref[at + (1,)])


def put(ref, value, *at):
    ref[at + (0,)] = value[0]
    ref[at + (1,)] = value[1]


def loop(low, high, body, carry, by):
    by = by if (high - low) % by == 0 else 1

    def several(k, carry):
        for i in range(by):
            carry = body(low + k * by + i, carry)
        return carry

    return lax.fori_loop(0, (high - low) // by, several, carry)


def rotation(angles, shape):
    cos = [jnp.cos(jnp.full(shape, angles[i], jnp.float32)) for i in range(3)]
    sin = [jnp.sin(jnp.full(shape, angles[i], jnp.float32)) for i in range(3)]
    (ca, cb, cc), (sa, sb, sc) = cos, sin
    left = [[ca * cb, -sa, ca * sb], [sa * cb, ca, sa * sb], [-sb, jnp.zeros_like(cb), cb]]
    return [[row[0] * cc + row[1] * sc, row[1] * cc - row[0] * sc, row[2]] for row in left]


def relax(
    ngz,
    nxy,
    field,
    source,
    classes,
    boundary,
    conductance,
    angles,
    strengths,
    OUT,
    U,
    S,
    C,
    B,
    SG,
    DR,
    PH,
    PHI,
    PSI,
    T,
    QM,
    EPHI,
    EPSI,
    EH,
    ET,
    ends,
    coef,
    near,
    halo_out,
    halo_in,
    value_in,
    info_in,
    info_out,
    lam_in,
    lam_out,
    extra_in,
    extra_out,
    own_in,
    own_out,
    ch_in,
    ch_out,
    in_sems,
    halo_send,
    halo_recv,
    info_send,
    info_recv,
    lam_send,
    lam_recv,
    extra_send,
    extra_recv,
    own_send,
    own_recv,
    ch_send,
    ch_recv,
):
    ix, iz = lax.axis_index("xy"), lax.axis_index("gz")
    depth, _, _, rows, width = U.shape
    kinds = conductance.shape[0]
    plane = (rows, width)
    has = {
        ("xy", 0): ix > 0,
        ("xy", 1): ix < nxy - 1,
    }
    where_is = {
        ("xy", 0): ix - 1,
        ("xy", 1): ix + 1,
    }
    for steps in (1, 2):
        has["gz", -steps] = iz >= steps
        has["gz", steps] = iz < ngz - steps
        where_is["gz", -steps] = iz - steps
        where_is["gz", steps] = iz + steps
    zs = depth // PIECES
    spans = [pl.ds(piece * zs, zs) for piece in range(PIECES)]
    moves = [(field.at[span], U.at[span]) for span in spans]
    moves += [(classes, C), (boundary, B), (source, S)]
    loads = [
        pltpu.make_async_copy(src, dst, in_sems.at[i]) for i, (src, dst) in enumerate(moves)
    ]
    for load in loads[:-1]:
        load.start()

    barrier = pltpu.get_barrier_semaphore()
    for key, there in has.items():

        @pl.when(there)
        def _():
            pl.semaphore_signal(
                barrier,
                inc=1,
                device_id={key[0]: where_is[key]},
                device_id_type=pl.DeviceIdType.MESH,
            )


    def remote(src, dst, send, recv, key):
        return pltpu.make_async_remote_copy(
            src_ref=src,
            dst_ref=dst,
            send_sem=send,
            recv_sem=recv,
            device_id={key[0]: where_is[key]},
            device_id_type=pl.DeviceIdType.MESH,
        )

    def halo_copy(sweep, side, piece):
        span = pl.ds(piece * zs, zs)
        return remote(
            halo_out.at[sweep, side, :, :, span],
            halo_in.at[sweep, side, :, :, span],
            halo_send.at[sweep, side, piece],
            halo_recv.at[sweep, side, piece],
            ("xy", 1 - side),
        )

    def send_halo(sweep, piece):
        for side in range(2):

            @pl.when(has["xy", 1 - side])
            def _():
                halo_copy(sweep, side, piece).start()

    def pack(first, last, z, values):
        for i in range(6):
            at = (i // 3, i % 3, pl.ds(z, 1), slice(None))
            first[at] = values[i][:1, :]
            last[at] = values[i][rows - 1 :, :]

    for side in range(2):

        @pl.when(jnp.logical_not(has["xy", side]))
        def _():
            for sweep in range(SWEEPS):
                halo_in[sweep, side] = jnp.zeros(halo_in.shape[2:], jnp.float32)

        @pl.when((iz if side == 0 else ngz - 1 - iz) < 2)
        def _():
            for part in range(3, 9):
                info_in[side, part] = jnp.zeros(info_in.shape[2:], jnp.float32)
            extra_in[side] = jnp.zeros(extra_in.shape[1:], jnp.float32)
            lam_in[side] = jnp.zeros(lam_in.shape[1:], jnp.float32)
            for sweep in range(SWEEPS):
                for j in range(3):
                    ch_in[sweep, side, j] = jnp.zeros(ch_in.shape[3:], jnp.float32)

    count = sum(there.astype(jnp.int32) for there in has.values())

    def pack_first(z, carry):
        values = [U[z, i // 3, i % 3] for i in range(6)]
        pack(halo_out.at[0, 1], halo_out.at[0, 0], z, values)
        return carry

    for piece in range(PIECES):
        loads[piece].wait()
        if piece == PIECES - 1:
            loads[-1].start()
        loop(piece * zs, (piece + 1) * zs, pack_first, 0, 4)
        if piece == 0:
            pl.semaphore_wait(barrier, count)
        send_halo(0, piece)

    loads[PIECES].wait()
    loads[PIECES + 1].wait()

    def diagonal(z, carry):
        ids = C[z]
        sigma = jnp.zeros(plane, jnp.float32)
        for kind in range(kinds):
            sigma = jnp.where(ids == kind, conductance[kind], sigma)
        SG[z] = sigma
        DR[z] = 2.0 + 4.0 * coupling + penalty * B[z].astype(jnp.float32)
        return carry

    loop(0, depth, diagonal, 0, 4)

    def diag(z):
        real = jnp.broadcast_to(DR[z][None], (3,) + plane)
        sigma = SG[z]
        return real, jnp.stack([sigma * strengths[j] for j in range(3)])

    none = (jnp.zeros((3,) + plane, jnp.float32),) * 2

    def pivots(k, carry):
        p, q = carry
        z, back = k, depth - 1 - k
        d, f = diag(z), diag(back)
        p = inv((d[0] - p[0], d[1] - p[1]))
        q = inv((f[0] - q[0], f[1] - q[1]))
        put(PH, p, z)
        put(PHI, q, back)
        return p, q

    loop(0, depth, pivots, (none, none), 2)
    ones = (jnp.ones((3,) + plane, jnp.float32), none[0])

    def columns(k, carry):
        down, up = carry
        z, back = k, depth - 1 - k
        down = mul(get(PHI, z), down)
        up = mul(get(PH, back), up)
        put(PHI, down, z)
        put(PSI, up, back)
        return down, up

    loop(0, depth, columns, (ones, ones), 2)
    LEFT, RIGHT = 0, 1
    tip = (lambda: get(PHI, 0), lambda: get(PSI, depth - 1))
    across = lambda: get(PSI, 0)

    place = (iz, ngz - 1 - iz)
    even = [lax.rem(k, 2) == 0 for k in place]
    odd = [lax.rem(k, 2) == 1 for k in place]
    onward = [ngz - 1 - k for k in place]

    def to(side, steps):
        return {"gz": iz + steps if side == LEFT else iz - steps}

    def chain_copy(src, dst, send, recv, side, steps):
        return pltpu.make_async_remote_copy(
            src_ref=src,
            dst_ref=dst,
            send_sem=send,
            recv_sem=recv,
            device_id=to(side, steps),
            device_id_type=pl.DeviceIdType.MESH,
        )

    def info_copy(side, j):
        return chain_copy(
            info_out.at[side, j],
            info_in.at[side, j],
            info_send.at[side, j],
            info_recv.at[side, j],
            side,
            1,
        )

    def lam_copy(side, steps, j):
        return chain_copy(
            lam_out.at[side, j],
            lam_in.at[side, j],
            lam_send.at[side, steps - 1, j],
            lam_recv.at[side, j],
            side,
            steps,
        )

    def own_copy(sweep, side, j):
        return chain_copy(
            own_out.at[sweep, side, j],
            own_in.at[sweep, side, j],
            own_send.at[sweep, side, j],
            own_recv.at[sweep, side, j],
            side,
            1,
        )

    def x_copy(sweep, side, steps, j):
        return chain_copy(
            ch_out.at[sweep, side, j],
            ch_in.at[sweep, side, j],
            ch_send.at[sweep, side, steps - 1, j],
            ch_recv.at[sweep, side, j],
            side,
            steps,
        )

    both = jnp.logical_and

    def send_info(side):
        parts = (tip[1 - side](), tip[side](), across())
        for part in range(3):
            for j in range(3):
                for p in range(2):
                    info_out[side, part * 3 + j, p] = parts[part][p][j]
            sends = both(even[side], onward[side] >= 1)

            @pl.when(sends if part == 0 else both(sends, place[side] > 0))
            def _():
                for j in range(3):
                    info_copy(side, part * 3 + j).start()

    def pass_lam(side):
        @pl.when(odd[side])
        def _():
            for j in range(3):
                info_copy(side, j).wait_recv()

        @pl.when(both(odd[side], place[side] >= 2))
        def _():
            for j in range(3, 9):
                info_copy(side, j).wait_recv()

        @pl.when(place[side] >= 2)
        def _():
            for j in range(3):
                lam_copy(side, 1, j).wait_recv()

        for j in range(3):
            tips = [(info_in[side, 3 * k + j, 0], info_in[side, 3 * k + j, 1]) for k in range(3)]
            given = (lam_in[side, j, 0], lam_in[side, j, 1])

            @pl.when(odd[side])
            def _():
                skip = mul(tips[2], inv(one_minus(mul(tips[1], given))))
                along = mul(skip, given)
                lam = add(tips[0], mul(tips[2], along))
                for p in range(2):
                    coef[12 + side, p, j] = along[p]
                    coef[8 + side, p, j] = skip[p]
                    coef[10 + side, p, j] = lam[p]

            @pl.when(even[side])
            def _():
                for p in range(2):
                    coef[10 + side, p, j] = given[p]

            of = lambda pair: (pair[0][j], pair[1][j])
            lam = (coef[10 + side, 0, j], coef[10 + side, 1, j])
            kappa = mul(of(across()), inv(one_minus(mul(of(tip[side]()), lam))))
            over = mul(kappa, lam)
            value = add(of(tip[1 - side]()), mul(of(across()), over))
            for p in range(2):
                coef[side, p, j] = kappa[p]
                coef[2 + side, p, j] = over[p]
                lam_out[side, j, p] = value[p]

            @pl.when(both(odd[side], onward[side] >= 2))
            def _():
                lam_copy(side, 2, j).start()

        @pl.when(both(odd[side], onward[side] >= 1))
        def _():
            for j in range(3):
                lam_copy(side, 1, j).start()

    def extra_copy(side, j):
        return chain_copy(
            extra_out.at[side, j],
            extra_in.at[side, j],
            extra_send.at[side, j],
            extra_recv.at[side, j],
            side,
            1,
        )

    def own_base(side, j):
        return add(
            (ends[1 - side, 0, j], ends[1 - side, 1, j]),
            mul(
                (coef[2 + side, 0, j], coef[2 + side, 1, j]),
                (ends[side, 0, j], ends[side, 1, j]),
            ),
        )

    def own_sum(sweep, side):
        for j in range(3):
            if sweep == 0:
                for p in range(2):
                    own_out[sweep, side, j, p] = ends[1 - side, p, j]
                    extra_out[side, j, p] = ends[side, p, j]
            else:
                base = own_base(side, j)
                for p in range(2):
                    own_out[sweep, side, j, p] = base[p]
            sends = both(even[side], onward[side] >= 1)

            @pl.when(sends)
            def _():
                own_copy(sweep, side, j).start()

            if sweep == 0:

                @pl.when(both(sends, place[side] > 0))
                def _():
                    extra_copy(side, j).start()

    def pass_chain(sweep, side):
        for j in range(3):
            base = own_base(side, j)

            @pl.when(odd[side])
            def _():
                own_copy(sweep, side, j).wait_recv()

            if sweep == 0:

                @pl.when(both(odd[side], place[side] >= 2))
                def _():
                    extra_copy(side, j).wait_recv()

            @pl.when(place[side] >= 2)
            def _():
                x_copy(sweep, side, 1, j).wait_recv()

            given = (ch_in[sweep, side, j, 0], ch_in[sweep, side, j, 1])

            @pl.when(odd[side])
            def _():
                own = (own_in[sweep, side, j, 0], own_in[sweep, side, j, 1])
                if sweep == 0:
                    extra = (extra_in[side, j, 0], extra_in[side, j, 1])
                    own = add(own, mul((coef[12 + side, 0, j], coef[12 + side, 1, j]), extra))
                x = add(own, mul((coef[8 + side, 0, j], coef[8 + side, 1, j]), given))
                for p in range(2):
                    value_in[side, j, p] = x[p]

            @pl.when(even[side])
            def _():
                for p in range(2):
                    value_in[side, j, p] = given[p]

            x = (value_in[side, j, 0], value_in[side, j, 1])
            result = add(base, mul((coef[side, 0, j], coef[side, 1, j]), x))
            for p in range(2):
                ch_out[sweep, side, j, p] = result[p]

            @pl.when(both(odd[side], onward[side] >= 2))
            def _():
                x_copy(sweep, side, 2, j).start()

        @pl.when(both(odd[side], onward[side] >= 1))
        def _():
            for j in range(3):
                x_copy(sweep, side, 1, j).start()

    left_first = iz * 2 < ngz - 1

    def near_side(run):
        @pl.when(left_first)
        def _():
            run(LEFT)

        @pl.when(jnp.logical_not(left_first))
        def _():
            run(RIGHT)

    def far_side(run):
        @pl.when(left_first)
        def _():
            run(RIGHT)

        @pl.when(jnp.logical_not(left_first))
        def _():
            run(LEFT)

    near_side(send_info)
    far_side(send_info)

    angle_matrix = rotation(angles, (rows, 128))
    for c in range(3):
        for j in range(3):
            QM[c, j] = angle_matrix[c][j]

    def matrix():
        return [
            [jnp.concatenate([QM[c, j]] * (width // 128), axis=1) for j in range(3)]
            for c in range(3)
        ]

    def pack_columns(z, carry):
        for src, dst in ((PHI, EPHI), (PSI, EPSI)):
            pack(dst.at[0], dst.at[1], z, [src[z, i // 3, i % 3] for i in range(6)])
        return carry

    loop(0, depth, pack_columns, 0, 4)

    row = lax.broadcasted_iota(jnp.int32, plane, 0)
    lane = lax.broadcasted_iota(jnp.int32, plane, 1)
    zero = jnp.zeros(plane, jnp.float32)

    def turn(q, driven):
        return [
            jnp.stack(
                [
                    q[0][j] * driven[p][0] + q[1][j] * driven[p][1] + q[2][j] * driven[p][2]
                    for j in range(3)
                ]
            )
            for p in range(2)
        ]

    def inner(z, carry):
        first, last = carry
        q = matrix()
        driven = []
        for p in range(2):
            of = []
            for c in range(3):
                u = U[z, p, c]
                beside = jnp.where(lane == 0, zero, pltpu.roll(u, 1, 1))
                beside += jnp.where(lane == width - 1, zero, pltpu.roll(u, width - 1, 1))
                beside += jnp.where(row == 0, zero, pltpu.roll(u, 1, 0))
                beside += jnp.where(row == rows - 1, zero, pltpu.roll(u, rows - 1, 0))
                of.append(S[z, p, c] + coupling * beside)
            driven.append(of)
        turned = turn(q, driven)
        put(T, turned, z)
        return add(first, mul(get(PHI, z), turned)), add(last, mul(get(PSI, z), turned))

    tiles = [pl.ds(z, rows) for z in range(0, depth, rows)]

    def outer(sweep, side, tile, carry):
        first, last = carry
        q = matrix()
        turned = turn(
            q,
            [[coupling * halo_in[sweep, side, p, c, tile] for c in range(3)] for p in range(2)],
        )
        for p in range(2):
            EH[side, p, :, tile] = turned[p]
        phi = [EPHI[side, p, :, tile] for p in range(2)]
        psi = [EPSI[side, p, :, tile] for p in range(2)]
        return add(first, mul(phi, turned)), add(last, mul(psi, turned))

    loads[PIECES + 2].wait()
    for sweep in range(SWEEPS):
        sums = loop(0, depth, inner, (none, none), 4)
        if sweep == 0:
            near_side(pass_lam)
        halves = [(none, none), (none, none)]
        for piece in range(PIECES):
            for side in range(2):

                @pl.when(has["xy", side])
                def _():
                    halo_copy(sweep, side, piece).wait_recv()

                for tile in tiles[piece * len(tiles) // PIECES : (piece + 1) * len(tiles) // PIECES]:
                    halves[side] = outer(sweep, side, tile, halves[side])
        for side in range(2):
            here = row == (0 if side == 0 else rows - 1)
            sums = tuple(
                add(
                    sums[end],
                    tuple(
                        jnp.where(here[None], jnp.sum(part, axis=1, keepdims=True), 0.0)
                        for part in halves[side][end]
                    ),
                )
                for end in range(2)
            )
        put(ends, sums[0], 0)
        put(ends, sums[1], 1)

        near_side(functools.partial(own_sum, sweep))
        far_side(functools.partial(own_sum, sweep))
        near_side(functools.partial(pass_chain, sweep))

        def forward(z, m):
            given = []
            for p in range(2):
                edges = []
                for j in range(3):
                    above = jnp.broadcast_to(EH[0, p, j, pl.ds(z, 1), :], plane)
                    below = jnp.broadcast_to(EH[1, p, j, pl.ds(z, 1), :], plane)
                    edges.append(
                        jnp.where(row == 0, above, zero) + jnp.where(row == rows - 1, below, zero)
                    )
                given.append(T[z, p] + jnp.stack(edges))
            m = mul(get(PH, z), add(given, m))
            put(T, m, z)
            return m

        def backward(k, w):
            z = depth - 1 - k
            w = add(get(T, z), mul(get(PH, z), w))
            put(T, w, z)
            if sweep < SWEEPS - 1:
                pack(ET.at[0], ET.at[1], z, [w[i // 3][i % 3] for i in range(6)])
            return w

        loop(0, depth, forward, none, 4)
        loop(0, depth, backward, none, 4)
        if sweep == 0:
            far_side(pass_lam)
            for side in range(2):
                lam = get(coef, 10 + side)
                away = tuple(
                    jnp.stack([lam_out[1 - side, j, p] for j in range(3)]) for p in range(2)
                )
                det = inv(one_minus(mul(lam, away)))
                put(coef, det, 6 + side)
                put(coef, mul(det, lam), 4 + side)
        far_side(functools.partial(pass_chain, sweep))

        for side in range(2):
            for j in range(3):
                arrived = (value_in[side, j, 0], value_in[side, j, 1])
                other = (ch_out[sweep, 1 - side, j, 0], ch_out[sweep, 1 - side, j, 1])
                value = add(
                    mul((coef[6 + side, 0, j], coef[6 + side, 1, j]), arrived),
                    mul((coef[4 + side, 0, j], coef[4 + side, 1, j]), other),
                )
                near[side, 0, j] = value[0]
                near[side, 1, j] = value[1]

        final = sweep == SWEEPS - 1

        def join_edge(side, tile):
            q = matrix()
            r = 0 if side == 0 else rows - 1
            w = [ET[side, p, :, tile] for p in range(2)]
            for end, column in ((0, EPHI), (1, EPSI)):
                entry = [
                    jnp.broadcast_to(near[end, p, :, r : r + 1, :], (3,) + plane)
                    for p in range(2)
                ]
                w = add(w, mul([column[side, p, :, tile] for p in range(2)], entry))
            for p in range(2):
                for c in range(3):
                    halo_out[sweep + 1, 1 - side, p, c, tile] = (
                        q[c][0] * w[p][0] + q[c][1] * w[p][1] + q[c][2] * w[p][2]
                    )

        if not final:
            for piece in range(PIECES):
                for tile in tiles[piece * len(tiles) // PIECES : (piece + 1) * len(tiles) // PIECES]:
                    for side in range(2):
                        join_edge(side, tile)
                send_halo(sweep + 1, piece)


        def join(z, carry):
            q = matrix()
            before, after = get(near, 0), get(near, 1)
            w = add(add(get(T, z), mul(get(PHI, z), before)), mul(get(PSI, z), after))
            values = []
            for p in range(2):
                for c in range(3):
                    values.append(q[c][0] * w[p][0] + q[c][1] * w[p][1] + q[c][2] * w[p][2])
            target = OUT if final else U
            for i in range(6):
                target[z, i // 3, i % 3] = values[i]
            return carry

        loop(0, depth, join, 0, 4)

    for side in range(2):

        @pl.when(has["xy", 1 - side])
        def _():
            for sweep in range(SWEEPS):
                for piece in range(PIECES):
                    halo_copy(sweep, side, piece).wait_send()

        sends = both(even[side], onward[side] >= 1)

        @pl.when(sends)
        def _():
            for j in range(3):
                info_copy(side, j).wait_send()
                for sweep in range(SWEEPS):
                    own_copy(sweep, side, j).wait_send()

        @pl.when(both(sends, place[side] > 0))
        def _():
            for j in range(3, 9):
                info_copy(side, j).wait_send()
            for j in range(3):
                extra_copy(side, j).wait_send()

        for steps in (2, 1):

            @pl.when(both(odd[side], onward[side] >= steps))
            def _():
                for j in range(3):
                    lam_copy(side, steps, j).wait_send()
                    for sweep in range(SWEEPS):
                        x_copy(sweep, side, steps, j).wait_send()


def local(ngz, nxy, field, source, classes, boundary, conductance, angles, strengths):
    depth, _, _, rows, width = field.shape
    f32 = jnp.float32
    block = pltpu.VMEM(field.shape, f32)
    flat = (depth, rows, width)
    line = (2, 3, rows, width)
    pair = (2, rows, width)
    edge = (2, 2, 3, depth, width)
    dma = pltpu.SemaphoreType.DMA
    hbm = pl.BlockSpec(memory_space=pl.ANY)
    smem = pl.BlockSpec(memory_space=pltpu.SMEM)
    return pl.pallas_call(
        functools.partial(relax, ngz, nxy),
        out_shape=pltpu.VMEM(field.shape, f32),
        in_specs=[hbm] * 4 + [smem] * 3,
        out_specs=pl.BlockSpec(memory_space=pltpu.VMEM),
        scratch_shapes=[
            block,
            block,
            pltpu.VMEM(flat, jnp.int32),
            pltpu.VMEM(flat, jnp.int32),
            pltpu.VMEM(flat, f32),
            pltpu.VMEM(flat, f32),
            block,
            block,
            block,
            block,
            pltpu.VMEM((3, 3, rows, 128), f32),
            pltpu.VMEM(edge, f32),
            pltpu.VMEM(edge, f32),
            pltpu.VMEM(edge, f32),
            pltpu.VMEM(edge, f32),
            pltpu.VMEM((2,) + line, f32),
            pltpu.VMEM((14,) + line, f32),
            pltpu.VMEM((2,) + line, f32),
            pltpu.VMEM((SWEEPS,) + edge, f32),
            pltpu.VMEM((SWEEPS,) + edge, f32),
            pltpu.VMEM((2, 3) + pair, f32),
            pltpu.VMEM((2, 9) + pair, f32),
            pltpu.VMEM((2, 9) + pair, f32),
            pltpu.VMEM((2, 3) + pair, f32),
            pltpu.VMEM((2, 3) + pair, f32),
            pltpu.VMEM((2, 3) + pair, f32),
            pltpu.VMEM((2, 3) + pair, f32),
            pltpu.VMEM((SWEEPS, 2, 3) + pair, f32),
            pltpu.VMEM((SWEEPS, 2, 3) + pair, f32),
            pltpu.VMEM((SWEEPS, 2, 3) + pair, f32),
            pltpu.VMEM((SWEEPS, 2, 3) + pair, f32),
            dma((PIECES + 3,)),
            dma((SWEEPS, 2, PIECES)),
            dma((SWEEPS, 2, PIECES)),
            dma((2, 9)),
            dma((2, 9)),
            dma((2, 2, 3)),
            dma((2, 3)),
            dma((2, 3)),
            dma((2, 3)),
            dma((SWEEPS, 2, 3)),
            dma((SWEEPS, 2, 3)),
            dma((SWEEPS, 2, 2, 3)),
            dma((SWEEPS, 2, 3)),
        ],
        compiler_params=pltpu.CompilerParams(collective_id=0, has_side_effects=True, vmem_limit_bytes=VMEM_LIMIT),
    )(field, source, classes, boundary, conductance, angles, strengths)


def solution(mesh):
    in_specs = (
        P("gz", None, None, "xy", None),
        P("gz", None, None, "xy", None),
        P("gz", "xy", None),
        P("gz", "xy", None),
        P(),
        P(),
        P(),
    )
    out_specs = P("gz", None, None, "xy", None)
    body = functools.partial(local, mesh.shape["gz"], mesh.shape["xy"])
    return jax.shard_map(body, mesh=mesh, in_specs=in_specs, out_specs=out_specs, check_vma=False)
```

profile of v0, /device:TPU:31, one launch (start us, length us, event | category | flops | bytes accessed | tf_op | source)
XLA Modules:
  0.0 36.5 jit_solution(14984433688927136980)
XLA Ops:
  0.0 35.6 %shard_map.73 = f32[16,2,3,8,256]{4,3,2,1,0:T(8,128)S(1)} custom-call(f32[16,2,3,8,256]{4,3,2,1,0:T(8,128)} %field.1, f32[16,2,3,8,256]{4,3,2,1,0:T(8,128)} %source.1, s32[16,8,256]{2,1,0:T(8,128)} %classes.1, s32[16,8,256]{2,1,0:T(8,128)} %boundary.1, f32[16]{0:T(128)} %conductance.1, f32[3]{0:T(128)} %angles.1, f32[3]{0:T(128)} %strengths.1), custom_call_target="tpu_custom_call" | custom-call | tf_op jit(solution)/shard_map/pallas_call | solution.py:747
  35.7 0.9 %copy.9 = f32[16,2,3,8,256]{4,3,2,1,0:T(8,128)} copy(f32[16,2,3,8,256]{4,3,2,1,0:T(8,128)S(1)} %shard_map.73) | data formatting | bytes 1572864
where the time goes:
time: 36.6 us; the launch traced here: 36.5 us
  Pallas kernels  35.6 us (97%)
  local copies, waits for them, and re-layouts  0.88 us (2%)
    pallas_call x1, Pallas kernels, local(): pl.pallas_call(functools.partial(relax, ngz, nxy), out_shape=pltpu.VMEM(f...  35.6 us
    unnamed x1, local copies, waits for them, and re-layouts  0.88 us

commit v1 on v0

--- a/solution.py
+++ b/solution.py
@@ -102,6 +102,17 @@
     own_out,
     ch_in,
     ch_out,
+    XR,
+    CX,
+    BX,
+    FP,
+    FPHI,
+    FPSI,
+    FT,
+    FC,
+    far_ends,
+    mi_in,
+    mi_out,
     in_sems,
     halo_send,
     halo_recv,
@@ -115,6 +126,11 @@
     own_recv,
     ch_send,
     ch_recv,
+    far_local,
+    far_send,
+    far_recv,
+    mi_send,
+    mi_recv,
 ):
     ix, iz = lax.axis_index("xy"), lax.axis_index("gz")
     depth, _, _, rows, width = U.shape
@@ -128,10 +144,18 @@
         ("xy", 0): ix - 1,
         ("xy", 1): ix + 1,
     }
+    middle = nxy // 2
+    far = (ix == middle, ix == middle - 1)
+    is_far = jnp.logical_or(far[0], far[1])
+    not_far = jnp.logical_not(is_far)
+    beside = [jnp.logical_and(has["xy", side], jnp.logical_not(far[side])) for side in range(2)]
     for steps in (1, 2):
         has["gz", -steps] = iz >= steps
         has["gz", steps] = iz < ngz - steps
         where_is["gz", -steps] = iz - steps
+        where_is["gz", steps] = iz + steps
+    for steps in (-3, 3):
+        has["gz", steps] = jnp.logical_and(is_far, (iz + steps >= 0) & (iz + steps < ngz))
         where_is["gz", steps] = iz + steps
     zs = depth // PIECES
     spans = [pl.ds(piece * zs, zs) for piece in range(PIECES)]
@@ -176,10 +200,11 @@
             ("xy", 1 - side),
         )
 
-    def send_halo(sweep, piece):
+    def send_halo(sweep, piece, given=None):
         for side in range(2):
-
-            @pl.when(has["xy", 1 - side])
+            there = has["xy", 1 - side] if sweep else jnp.logical_and(beside[1 - side], given)
+
+            @pl.when(there)
             def _():
                 halo_copy(sweep, side, piece).start()
 
@@ -191,9 +216,10 @@
 
     for side in range(2):
 
-        @pl.when(jnp.logical_not(has["xy", side]))
-        def _():
-            for sweep in range(SWEEPS):
+        for sweep in range(SWEEPS):
+
+            @pl.when(jnp.logical_not(has["xy", side] if sweep else beside[side]))
+            def _():
                 halo_in[sweep, side] = jnp.zeros(halo_in.shape[2:], jnp.float32)
 
         @pl.when((iz if side == 0 else ngz - 1 - iz) < 2)
@@ -219,8 +245,12 @@
             loads[-1].start()
         loop(piece * zs, (piece + 1) * zs, pack_first, 0, 4)
         if piece == 0:
-            pl.semaphore_wait(barrier, count)
-        send_halo(0, piece)
+
+            @pl.when(not_far)
+            def _():
+                pl.semaphore_wait(barrier, count)
+
+        send_halo(0, piece, not_far)
 
     loads[PIECES].wait()
     loads[PIECES + 1].wait()
@@ -507,6 +537,44 @@
         def _():
             run(LEFT)
 
+    def far_moves(side):
+        edge = pl.ds(rows - 1 if side else 0, 1)
+        to_far = {"xy": ix + 1 if side else ix - 1}
+        sources = [C.at[:, edge, :], B.at[:, edge, :]]
+        sources += [U.at[:, :, c, edge, :] for c in range(3)]
+        kept = [CX.at[:, 0:1, :], BX.at[:, 0:1, :]]
+        kept += [XR.at[:, :, 4 + c : 5 + c, :] for c in range(3)]
+        sent = [CX.at[:, 4:5, :], BX.at[:, 4:5, :]]
+        sent += [XR.at[:, :, c : c + 1, :] for c in range(3)]
+        remotes = [
+            pltpu.make_async_remote_copy(
+                src_ref=sources[i],
+                dst_ref=sent[i],
+                send_sem=far_send.at[i],
+                recv_sem=far_recv.at[i],
+                device_id=to_far,
+                device_id_type=pl.DeviceIdType.MESH,
+            )
+            for i in range(5)
+        ]
+        locals_ = [pltpu.make_async_copy(sources[i], kept[i], far_local.at[i]) for i in range(5)]
+        return remotes, locals_
+
+    @pl.when(is_far)
+    def _():
+        pl.semaphore_wait(barrier, count)
+
+    for side in range(2):
+
+        @pl.when(far[side])
+        def _():
+            remotes, locals_ = far_moves(side)
+            for copy in remotes + locals_:
+                copy.start()
+
+    for piece in range(PIECES):
+        send_halo(0, piece, is_far)
+
     near_side(send_info)
     far_side(send_info)
 
@@ -551,11 +619,11 @@
             of = []
             for c in range(3):
                 u = U[z, p, c]
-                beside = jnp.where(lane == 0, zero, pltpu.roll(u, 1, 1))
-                beside += jnp.where(lane == width - 1, zero, pltpu.roll(u, width - 1, 1))
-                beside += jnp.where(row == 0, zero, pltpu.roll(u, 1, 0))
-                beside += jnp.where(row == rows - 1, zero, pltpu.roll(u, rows - 1, 0))
-                of.append(S[z, p, c] + coupling * beside)
+                around = jnp.where(lane == 0, zero, pltpu.roll(u, 1, 1))
+                around += jnp.where(lane == width - 1, zero, pltpu.roll(u, width - 1, 1))
+                around += jnp.where(row == 0, zero, pltpu.roll(u, 1, 0))
+                around += jnp.where(row == rows - 1, zero, pltpu.roll(u, rows - 1, 0))
+                of.append(S[z, p, c] + coupling * around)
             driven.append(of)
         turned = turn(q, driven)
         put(T, turned, z)
@@ -576,6 +644,229 @@
         psi = [EPSI[side, p, :, tile] for p in range(2)]
         return add(first, mul(phi, turned)), add(last, mul(psi, turned))
 
+    third = lax.rem(row, 4)
+    part = lambda k: third == k
+    used = third < 3
+
+    def mi_copy(steps, stage):
+        slot = steps + 3 if steps < 0 else steps + 2
+        parts = pl.ds(0, 6) if stage == 0 else pl.ds(6, 4)
+        return pltpu.make_async_remote_copy(
+            src_ref=mi_out.at[parts],
+            dst_ref=mi_in.at[5 - slot, parts],
+            send_sem=mi_send.at[slot, stage],
+            recv_sem=mi_recv.at[5 - slot, stage],
+            device_id={"gz": iz + steps},
+            device_id_type=pl.DeviceIdType.MESH,
+        )
+
+    all_steps = (-3, -2, -1, 1, 2, 3)
+
+    def to_all(stage, act):
+        for steps in all_steps:
+
+            @pl.when((iz + steps >= 0) & (iz + steps < ngz))
+            def _():
+                act(mi_copy(steps, stage))
+
+    def from_all(stage):
+        for steps in all_steps:
+            slot = steps + 3 if steps < 0 else steps + 2
+
+            @pl.when((iz + steps >= 0) & (iz + steps < ngz))
+            def _():
+                pltpu.make_async_remote_copy(
+                    src_ref=mi_out.at[pl.ds(0, 6) if stage == 0 else pl.ds(6, 4)],
+                    dst_ref=mi_in.at[slot, pl.ds(0, 6) if stage == 0 else pl.ds(6, 4)],
+                    send_sem=mi_send.at[slot, stage],
+                    recv_sem=mi_recv.at[slot, stage],
+                    device_id={"gz": iz + steps},
+                    device_id_type=pl.DeviceIdType.MESH,
+                ).wait_recv()
+
+    def shifts(of):
+        planes = []
+        for d in (-2, -1, 0, 1, 2):
+            plane_ = zero
+            for j in range(3):
+                if 0 <= j + d <= 2:
+                    plane_ = jnp.where(part(j), of(j, j + d), plane_)
+            planes.append((d, plane_))
+        return planes
+
+    def mix(planes, x):
+        total = None
+        for d, plane_ in planes:
+            term = plane_ * (x if d == 0 else pltpu.roll(x, (rows - d) % rows, 0))
+            total = term if total is None else total + term
+        return total
+
+    def far_setup():
+        for slot, steps in enumerate(all_steps):
+
+            @pl.when(jnp.logical_not((iz + steps >= 0) & (iz + steps < ngz)))
+            def _():
+                mi_in[slot] = jnp.zeros(mi_in.shape[1:], jnp.float32)
+
+        q = matrix()
+        for i, (_, plane_) in enumerate(shifts(lambda j, k: q[k][j])):
+            FC[i] = plane_
+        for i, (_, plane_) in enumerate(shifts(lambda j, k: q[j][k])):
+            FC[5 + i] = plane_
+        strength = jnp.full(plane, strengths[0], jnp.float32)
+        for j in (1, 2):
+            strength = jnp.where(part(j), strengths[j], strength)
+        FC[10] = strength
+
+    def far_first():
+        for side in range(2):
+
+            @pl.when(far[side])
+            def _():
+                remotes, locals_ = far_moves(side)
+                for i in range(2):
+                    locals_[i].wait()
+                    remotes[i].wait_recv()
+
+        own = row < 4
+
+        def far_diagonal(z, carry):
+            ids_tile, bound = CX[z], BX[z]
+            ids = jnp.where(
+                own,
+                jnp.broadcast_to(ids_tile[0:1, :], plane),
+                jnp.broadcast_to(ids_tile[4:5, :], plane),
+            )
+            edge = jnp.where(
+                own, jnp.broadcast_to(bound[0:1, :], plane), jnp.broadcast_to(bound[4:5, :], plane)
+            )
+            sigma = jnp.zeros(plane, jnp.float32)
+            for kind in range(kinds):
+                sigma = jnp.where(ids == kind, conductance[kind], sigma)
+            FT[z, 0] = 2.0 + 4.0 * coupling + penalty * edge.astype(jnp.float32)
+            FT[z, 1] = sigma * FC[10]
+            return carry
+
+        loop(0, depth, far_diagonal, 0, 4)
+
+        def far_pivots(k, carry):
+            p, q = carry
+            d, f = get(FT, k), get(FT, depth - 1 - k)
+            p = inv((d[0] - p[0], d[1] - p[1]))
+            q = inv((f[0] - q[0], f[1] - q[1]))
+            put(FP, p, k)
+            put(FPHI, q, depth - 1 - k)
+            return p, q
+
+        loop(0, depth, far_pivots, ((zero, zero), (zero, zero)), 2)
+        one = jnp.ones(plane, jnp.float32)
+
+        def far_columns(k, carry):
+            down, up = carry
+            back = depth - 1 - k
+            down = mul(get(FPHI, k), down)
+            up = mul(get(FP, back), up)
+            put(FPHI, down, k)
+            put(FPSI, up, back)
+            return down, up
+
+        loop(0, depth, far_columns, ((one, zero), (one, zero)), 2)
+        for i, value in enumerate((get(FPHI, 0), get(FPSI, depth - 1), get(FPSI, 0))):
+            mi_out[2 * i] = value[0]
+            mi_out[2 * i + 1] = value[1]
+        to_all(0, lambda copy: copy.start())
+
+    def far_second():
+        for side in range(2):
+
+            @pl.when(far[side])
+            def _():
+                remotes, locals_ = far_moves(side)
+                for i in range(2, 5):
+                    remotes[i].wait_recv()
+
+        turned_by = [(d, FC[i]) for i, d in enumerate((-2, -1, 0, 1, 2))]
+
+        def far_sums(z, carry):
+            first, last = carry
+            t = tuple(
+                mix(turned_by, jnp.where(used, coupling * XR[z, p], zero)) for p in range(2)
+            )
+            put(FT, t, z)
+            return add(first, mul(get(FPHI, z), t)), add(last, mul(get(FPSI, z), t))
+
+        first, last = loop(0, depth, far_sums, ((zero, zero), (zero, zero)), 4)
+        for i, value in enumerate((first, last)):
+            mi_out[6 + 2 * i] = value[0]
+            mi_out[7 + 2 * i] = value[1]
+        to_all(1, lambda copy: copy.start())
+
+        def far_forward(z, m):
+            m = mul(get(FP, z), add(get(FT, z), m))
+            put(FT, m, z)
+            return m
+
+        def far_backward(k, w):
+            z = depth - 1 - k
+            w = add(get(FT, z), mul(get(FP, z), w))
+            put(FT, w, z)
+            return w
+
+        loop(0, depth, far_forward, (zero, zero), 4)
+        loop(0, depth, far_backward, (zero, zero), 4)
+
+    def far_third():
+        from_all(0)
+        from_all(1)
+        block = lambda slot: [(mi_in[slot, 2 * i], mi_in[slot, 2 * i + 1]) for i in range(5)]
+        x = lam = y = mu = (zero, zero)
+        for slot in range(3):
+            top, bottom, cross, first, last = block(slot)
+            det = inv(one_minus(mul(top, lam)))
+            x, lam = (
+                add(last, mul(cross, mul(det, add(x, mul(lam, first))))),
+                add(bottom, mul(mul(cross, cross), mul(det, lam))),
+            )
+        for slot in (5, 4, 3):
+            top, bottom, cross, first, last = block(slot)
+            det = inv(one_minus(mul(bottom, mu)))
+            y, mu = (
+                add(first, mul(cross, mul(det, add(y, mul(mu, last))))),
+                add(top, mul(mul(cross, cross), mul(det, mu))),
+            )
+        top, bottom, cross, first, last = [(mi_out[2 * i], mi_out[2 * i + 1]) for i in range(5)]
+        g, h = add(x, mul(lam, first)), add(y, mul(mu, last))
+        alpha, beta = one_minus(mul(lam, top)), one_minus(mul(mu, bottom))
+        lc, mc = mul(lam, cross), mul(mu, cross)
+        both_ = mul(lc, mc)
+        whole = mul(alpha, beta)
+        det = inv((whole[0] - both_[0], whole[1] - both_[1]))
+        put(far_ends, mul(det, add(mul(g, beta), mul(lc, h))), 0)
+        put(far_ends, mul(det, add(mul(h, alpha), mul(mc, g))), 1)
+        back_by = [(d, FC[5 + i]) for i, d in enumerate((-2, -1, 0, 1, 2))]
+        here = row == jnp.where(far[1], rows - 1, 0)
+
+        def far_join(z, carry):
+            before, after = get(far_ends, 0), get(far_ends, 1)
+            w = add(add(get(FT, z), mul(get(FPHI, z), before)), mul(get(FPSI, z), after))
+            for p in range(2):
+                u = mix(back_by, w[p])
+                FT[z, p] = u
+                for c in range(3):
+                    U[z, p, c] += jnp.where(here, jnp.broadcast_to(u[c : c + 1, :], plane), zero)
+            return carry
+
+        loop(0, depth, far_join, 0, 4)
+
+    def add_far_row(side, piece):
+        def one_row(z, carry):
+            for p in range(2):
+                for c in range(3):
+                    halo_in[1, side, p, c, pl.ds(z, 1), :] += FT[z, p, 4 + c : 5 + c, :]
+            return carry
+
+        loop(piece * zs, (piece + 1) * zs, one_row, 0, 4)
+
     loads[PIECES + 2].wait()
     for sweep in range(SWEEPS):
         sums = loop(0, depth, inner, (none, none), 4)
@@ -585,9 +876,15 @@
         for piece in range(PIECES):
             for side in range(2):
 
-                @pl.when(has["xy", side])
+                @pl.when(has["xy", side] if sweep else beside[side])
                 def _():
                     halo_copy(sweep, side, piece).wait_recv()
+
+                if sweep:
+
+                    @pl.when(far[side])
+                    def _():
+                        add_far_row(side, piece)
 
                 for tile in tiles[piece * len(tiles) // PIECES : (piece + 1) * len(tiles) // PIECES]:
                     halves[side] = outer(sweep, side, tile, halves[side])
@@ -697,13 +994,38 @@
                 target[z, i // 3, i % 3] = values[i]
             return carry
 
+        if not final:
+            for side in range(2):
+
+                @pl.when(far[side])
+                def _():
+                    remotes, locals_ = far_moves(side)
+                    for copy in remotes:
+                        copy.wait_send()
+                    for copy in locals_[2:]:
+                        copy.wait()
+
         loop(0, depth, join, 0, 4)
 
+        if not final:
+
+            @pl.when(is_far)
+            def _():
+                far_setup()
+                far_first()
+                far_second()
+                far_third()
+
+    @pl.when(is_far)
+    def _():
+        for stage in range(2):
+            to_all(stage, lambda copy: copy.wait_send())
+
     for side in range(2):
-
-        @pl.when(has["xy", 1 - side])
-        def _():
-            for sweep in range(SWEEPS):
+        for sweep in range(SWEEPS):
+
+            @pl.when(has["xy", 1 - side] if sweep else beside[1 - side])
+            def _():
                 for piece in range(PIECES):
                     halo_copy(sweep, side, piece).wait_send()
 
@@ -741,6 +1063,7 @@
     line = (2, 3, rows, width)
     pair = (2, rows, width)
     edge = (2, 2, 3, depth, width)
+    narrow = pltpu.VMEM((depth, 2, rows, width), f32)
     dma = pltpu.SemaphoreType.DMA
     hbm = pl.BlockSpec(memory_space=pl.ANY)
     smem = pl.BlockSpec(memory_space=pltpu.SMEM)
@@ -781,6 +1104,17 @@
             pltpu.VMEM((SWEEPS, 2, 3) + pair, f32),
             pltpu.VMEM((SWEEPS, 2, 3) + pair, f32),
             pltpu.VMEM((SWEEPS, 2, 3) + pair, f32),
+            narrow,
+            pltpu.VMEM(flat, jnp.int32),
+            pltpu.VMEM(flat, jnp.int32),
+            narrow,
+            narrow,
+            narrow,
+            narrow,
+            pltpu.VMEM((11, rows, width), f32),
+            pltpu.VMEM((2,) + pair, f32),
+            pltpu.VMEM((6, 10, rows, width), f32),
+            pltpu.VMEM((10, rows, width), f32),
             dma((PIECES + 3,)),
             dma((SWEEPS, 2, PIECES)),
             dma((SWEEPS, 2, PIECES)),
@@ -794,6 +1128,11 @@
             dma((SWEEPS, 2, 3)),
             dma((SWEEPS, 2, 2, 3)),
             dma((SWEEPS, 2, 3)),
+            dma((5,)),
+            dma((5,)),
+            dma((5,)),
+            dma((6, 2)),
+            dma((6, 2)),
         ],
         compiler_params=pltpu.CompilerParams(collective_id=0, has_side_effects=True, vmem_limit_bytes=VMEM_LIMIT),
     )(field, source, classes, boundary, conductance, angles, strengths)

time: 36.6 us -> 35.9 us (0.981)
  the two profiles are of different devices: /device:TPU:31 before, /device:TPU:160 now
where the time goes in v1:
time: 35.9 us; the launch traced here: 35.8 us
  Pallas kernels  34.9 us (97%)
  local copies, waits for them, and re-layouts  0.88 us (2%)
    pallas_call x1, Pallas kernels, local(): pl.pallas_call(functools.partial(relax, ngz, nxy), out_shape=pltpu.VMEM(f...  34.9 us
    unnamed x1, local copies, waits for them, and re-layouts  0.88 us

profile of v1, /device:TPU:160, one launch (start us, length us, event | category | flops | bytes accessed | tf_op | source)
XLA Modules:
  0.0 35.8 jit_solution(10566384341625601665)
XLA Ops:
  0.0 34.9 %shard_map.73 = f32[16,2,3,8,256]{4,3,2,1,0:T(8,128)S(1)} custom-call(f32[16,2,3,8,256]{4,3,2,1,0:T(8,128)} %field.1, f32[16,2,3,8,256]{4,3,2,1,0:T(8,128)} %source.1, s32[16,8,256]{2,1,0:T(8,128)} %classes.1, s32[16,8,256]{2,1,0:T(8,128)} %boundary.1, f32[16]{0:T(128)} %conductance.1, f32[3]{0:T(128)} %angles.1, f32[3]{0:T(128)} %strengths.1), custom_call_target="tpu_custom_call" | custom-call | tf_op jit(solution)/shard_map/pallas_call | solution.py:1070
  34.9 0.9 %copy.9 = f32[16,2,3,8,256]{4,3,2,1,0:T(8,128)} copy(f32[16,2,3,8,256]{4,3,2,1,0:T(8,128)S(1)} %shard_map.73) | data formatting | bytes 1572864

commit v2 on v1

--- a/solution.py
+++ b/solution.py
@@ -96,8 +96,6 @@
     info_out,
     lam_in,
     lam_out,
-    extra_in,
-    extra_out,
     own_in,
     own_out,
     ch_in,
@@ -116,12 +114,12 @@
     in_sems,
     halo_send,
     halo_recv,
+    tip_send,
+    tip_recv,
     info_send,
     info_recv,
     lam_send,
     lam_recv,
-    extra_send,
-    extra_recv,
     own_send,
     own_recv,
     ch_send,
@@ -129,6 +127,9 @@
     far_local,
     far_send,
     far_recv,
+    near_ready,
+    row_send,
+    row_recv,
     mi_send,
     mi_recv,
 ):
@@ -148,15 +149,22 @@
     far = (ix == middle, ix == middle - 1)
     is_far = jnp.logical_or(far[0], far[1])
     not_far = jnp.logical_not(is_far)
+    helps = (ix == middle + 1, ix == middle - 2)
+    helper = jnp.logical_or(helps[0], helps[1])
+    pair = jnp.where(far[0], ix + 1, ix - 1)
     beside = [jnp.logical_and(has["xy", side], jnp.logical_not(far[side])) for side in range(2)]
     for steps in (1, 2):
         has["gz", -steps] = iz >= steps
         has["gz", steps] = iz < ngz - steps
         where_is["gz", -steps] = iz - steps
         where_is["gz", steps] = iz + steps
-    for steps in (-3, 3):
-        has["gz", steps] = jnp.logical_and(is_far, (iz + steps >= 0) & (iz + steps < ngz))
-        where_is["gz", steps] = iz + steps
+    signals = {}
+    for key, there in has.items():
+        signals[key] = jnp.logical_and(there, not_far)
+        if key[0] == "xy":
+            signals[key] = jnp.logical_and(signals[key], jnp.logical_not(helps[key[1]]))
+    count = sum(there.astype(jnp.int32) for there in signals.values())
+    count += ngz * helper.astype(jnp.int32)
     zs = depth // PIECES
     spans = [pl.ds(piece * zs, zs) for piece in range(PIECES)]
     moves = [(field.at[span], U.at[span]) for span in spans]
@@ -164,11 +172,11 @@
     loads = [
         pltpu.make_async_copy(src, dst, in_sems.at[i]) for i, (src, dst) in enumerate(moves)
     ]
-    for load in loads[:-1]:
+    for load in loads[PIECES : PIECES + 2] + loads[:PIECES] + loads[PIECES + 2 :]:
         load.start()
 
     barrier = pltpu.get_barrier_semaphore()
-    for key, there in has.items():
+    for key, there in signals.items():
 
         @pl.when(there)
         def _():
@@ -179,6 +187,22 @@
                 device_id_type=pl.DeviceIdType.MESH,
             )
 
+
+    @pl.when(is_far)
+    def _():
+        for g in range(ngz):
+            pl.semaphore_signal(
+                barrier,
+                inc=1,
+                device_id={"xy": pair, "gz": g},
+                device_id_type=pl.DeviceIdType.MESH,
+            )
+        pl.semaphore_signal(
+            barrier,
+            inc=1,
+            device_id={"xy": jnp.where(far[0], ix - 1, ix + 1)},
+            device_id_type=pl.DeviceIdType.MESH,
+        )
 
     def remote(src, dst, send, recv, key):
         return pltpu.make_async_remote_copy(
@@ -195,18 +219,35 @@
         return remote(
             halo_out.at[sweep, side, :, :, span],
             halo_in.at[sweep, side, :, :, span],
-            halo_send.at[sweep, side, piece],
-            halo_recv.at[sweep, side, piece],
+            halo_send.at[side, piece],
+            halo_recv.at[side, piece],
             ("xy", 1 - side),
         )
 
-    def send_halo(sweep, piece, given=None):
+    def send_halo(sweep, piece):
         for side in range(2):
-            there = has["xy", 1 - side] if sweep else jnp.logical_and(beside[1 - side], given)
-
-            @pl.when(there)
+
+            @pl.when(has["xy", 1 - side])
             def _():
                 halo_copy(sweep, side, piece).start()
+
+    def row_copy(side, p, c):
+        return remote(
+            U.at[:, p, c, 0 if side else rows - 1, :],
+            halo_in.at[0, side, p, c],
+            row_send.at[side],
+            row_recv.at[side],
+            ("xy", 1 - side),
+        )
+
+    row_copies = lambda side: [row_copy(side, p, c) for p in range(2) for c in range(3)]
+    rows_moved = lambda side: remote(
+        halo_in.at[0, side],
+        halo_in.at[0, side],
+        row_send.at[side],
+        row_recv.at[side],
+        ("xy", 1 - side),
+    )
 
     def pack(first, last, z, values):
         for i in range(6):
@@ -226,31 +267,9 @@
         def _():
             for part in range(3, 9):
                 info_in[side, part] = jnp.zeros(info_in.shape[2:], jnp.float32)
-            extra_in[side] = jnp.zeros(extra_in.shape[1:], jnp.float32)
             lam_in[side] = jnp.zeros(lam_in.shape[1:], jnp.float32)
             for sweep in range(SWEEPS):
-                for j in range(3):
-                    ch_in[sweep, side, j] = jnp.zeros(ch_in.shape[3:], jnp.float32)
-
-    count = sum(there.astype(jnp.int32) for there in has.values())
-
-    def pack_first(z, carry):
-        values = [U[z, i // 3, i % 3] for i in range(6)]
-        pack(halo_out.at[0, 1], halo_out.at[0, 0], z, values)
-        return carry
-
-    for piece in range(PIECES):
-        loads[piece].wait()
-        if piece == PIECES - 1:
-            loads[-1].start()
-        loop(piece * zs, (piece + 1) * zs, pack_first, 0, 4)
-        if piece == 0:
-
-            @pl.when(not_far)
-            def _():
-                pl.semaphore_wait(barrier, count)
-
-        send_halo(0, piece, not_far)
+                ch_in[sweep, side] = jnp.zeros(ch_in.shape[2:], jnp.float32)
 
     loads[PIECES].wait()
     loads[PIECES + 1].wait()
@@ -296,6 +315,33 @@
         return down, up
 
     loop(0, depth, columns, (ones, ones), 2)
+    for piece in range(PIECES):
+        loads[piece].wait()
+
+    @pl.when(not_far)
+    def _():
+        pl.semaphore_wait(barrier, count)
+
+    @pl.when(helper)
+    def _():
+        pl.semaphore_signal(
+            near_ready,
+            inc=1,
+            device_id={"xy": jnp.where(helps[0], ix - 1, ix + 1)},
+            device_id_type=pl.DeviceIdType.MESH,
+        )
+
+    @pl.when(is_far)
+    def _():
+        pl.semaphore_wait(near_ready, 1)
+
+    for side in range(2):
+
+        @pl.when(beside[1 - side])
+        def _():
+            for copy in row_copies(side):
+                copy.start()
+
     LEFT, RIGHT = 0, 1
     tip = (lambda: get(PHI, 0), lambda: get(PSI, depth - 1))
     across = lambda: get(PSI, 0)
@@ -318,12 +364,22 @@
             device_id_type=pl.DeviceIdType.MESH,
         )
 
-    def info_copy(side, j):
+    def tip_copy(side, j):
         return chain_copy(
             info_out.at[side, j],
             info_in.at[side, j],
-            info_send.at[side, j],
-            info_recv.at[side, j],
+            tip_send.at[side],
+            tip_recv.at[side, j],
+            side,
+            1,
+        )
+
+    def info_copy(side):
+        return chain_copy(
+            info_out.at[side, 3:9],
+            info_in.at[side, 3:9],
+            info_send.at[side],
+            info_recv.at[side],
             side,
             1,
         )
@@ -332,7 +388,7 @@
         return chain_copy(
             lam_out.at[side, j],
             lam_in.at[side, j],
-            lam_send.at[side, steps - 1, j],
+            lam_send.at[side, steps - 1],
             lam_recv.at[side, j],
             side,
             steps,
@@ -342,7 +398,7 @@
         return chain_copy(
             own_out.at[sweep, side, j],
             own_in.at[sweep, side, j],
-            own_send.at[sweep, side, j],
+            own_send.at[sweep, side],
             own_recv.at[sweep, side, j],
             side,
             1,
@@ -352,54 +408,57 @@
         return chain_copy(
             ch_out.at[sweep, side, j],
             ch_in.at[sweep, side, j],
-            ch_send.at[sweep, side, steps - 1, j],
+            ch_send.at[sweep, side, steps - 1],
             ch_recv.at[sweep, side, j],
             side,
             steps,
         )
 
+    whole = slice(None)
+
     both = jnp.logical_and
 
     def send_info(side):
+        sends = both(even[side], onward[side] >= 1)
         parts = (tip[1 - side](), tip[side](), across())
         for part in range(3):
             for j in range(3):
                 for p in range(2):
                     info_out[side, part * 3 + j, p] = parts[part][p][j]
-            sends = both(even[side], onward[side] >= 1)
-
-            @pl.when(sends if part == 0 else both(sends, place[side] > 0))
-            def _():
-                for j in range(3):
-                    info_copy(side, part * 3 + j).start()
+            if part == 0:
+
+                @pl.when(sends)
+                def _():
+                    for j in range(3):
+                        tip_copy(side, j).start()
+
+        @pl.when(both(sends, place[side] > 0))
+        def _():
+            info_copy(side).start()
 
     def pass_lam(side):
-        @pl.when(odd[side])
-        def _():
-            for j in range(3):
-                info_copy(side, j).wait_recv()
-
         @pl.when(both(odd[side], place[side] >= 2))
         def _():
-            for j in range(3, 9):
-                info_copy(side, j).wait_recv()
-
-        @pl.when(place[side] >= 2)
-        def _():
-            for j in range(3):
+            info_copy(side).wait_recv()
+
+        for j in range(3):
+
+            @pl.when(odd[side])
+            def _():
+                tip_copy(side, j).wait_recv()
+
+            @pl.when(place[side] >= 2)
+            def _():
                 lam_copy(side, 1, j).wait_recv()
 
-        for j in range(3):
             tips = [(info_in[side, 3 * k + j, 0], info_in[side, 3 * k + j, 1]) for k in range(3)]
             given = (lam_in[side, j, 0], lam_in[side, j, 1])
 
             @pl.when(odd[side])
             def _():
                 skip = mul(tips[2], inv(one_minus(mul(tips[1], given))))
-                along = mul(skip, given)
-                lam = add(tips[0], mul(tips[2], along))
+                lam = add(tips[0], mul(tips[2], mul(skip, given)))
                 for p in range(2):
-                    coef[12 + side, p, j] = along[p]
                     coef[8 + side, p, j] = skip[p]
                     coef[10 + side, p, j] = lam[p]
 
@@ -418,24 +477,14 @@
                 coef[2 + side, p, j] = over[p]
                 lam_out[side, j, p] = value[p]
 
-            @pl.when(both(odd[side], onward[side] >= 2))
-            def _():
+            @pl.when(both(odd[side], onward[side] >= 1))
+            def _():
+                lam_copy(side, 1, j).start()
+
+        @pl.when(both(odd[side], onward[side] >= 2))
+        def _():
+            for j in range(3):
                 lam_copy(side, 2, j).start()
-
-        @pl.when(both(odd[side], onward[side] >= 1))
-        def _():
-            for j in range(3):
-                lam_copy(side, 1, j).start()
-
-    def extra_copy(side, j):
-        return chain_copy(
-            extra_out.at[side, j],
-            extra_in.at[side, j],
-            extra_send.at[side, j],
-            extra_recv.at[side, j],
-            side,
-            1,
-        )
 
     def own_base(side, j):
         return add(
@@ -448,25 +497,13 @@
 
     def own_sum(sweep, side):
         for j in range(3):
-            if sweep == 0:
-                for p in range(2):
-                    own_out[sweep, side, j, p] = ends[1 - side, p, j]
-                    extra_out[side, j, p] = ends[side, p, j]
-            else:
-                base = own_base(side, j)
-                for p in range(2):
-                    own_out[sweep, side, j, p] = base[p]
-            sends = both(even[side], onward[side] >= 1)
-
-            @pl.when(sends)
+            base = own_base(side, j)
+            for p in range(2):
+                own_out[sweep, side, j, p] = base[p]
+
+            @pl.when(both(even[side], onward[side] >= 1))
             def _():
                 own_copy(sweep, side, j).start()
-
-            if sweep == 0:
-
-                @pl.when(both(sends, place[side] > 0))
-                def _():
-                    extra_copy(side, j).start()
 
     def pass_chain(sweep, side):
         for j in range(3):
@@ -476,12 +513,6 @@
             def _():
                 own_copy(sweep, side, j).wait_recv()
 
-            if sweep == 0:
-
-                @pl.when(both(odd[side], place[side] >= 2))
-                def _():
-                    extra_copy(side, j).wait_recv()
-
             @pl.when(place[side] >= 2)
             def _():
                 x_copy(sweep, side, 1, j).wait_recv()
@@ -491,9 +522,6 @@
             @pl.when(odd[side])
             def _():
                 own = (own_in[sweep, side, j, 0], own_in[sweep, side, j, 1])
-                if sweep == 0:
-                    extra = (extra_in[side, j, 0], extra_in[side, j, 1])
-                    own = add(own, mul((coef[12 + side, 0, j], coef[12 + side, 1, j]), extra))
                 x = add(own, mul((coef[8 + side, 0, j], coef[8 + side, 1, j]), given))
                 for p in range(2):
                     value_in[side, j, p] = x[p]
@@ -537,43 +565,48 @@
         def _():
             run(LEFT)
 
-    def far_moves(side):
+    def far_source(side, i):
         edge = pl.ds(rows - 1 if side else 0, 1)
-        to_far = {"xy": ix + 1 if side else ix - 1}
-        sources = [C.at[:, edge, :], B.at[:, edge, :]]
-        sources += [U.at[:, :, c, edge, :] for c in range(3)]
-        kept = [CX.at[:, 0:1, :], BX.at[:, 0:1, :]]
-        kept += [XR.at[:, :, 4 + c : 5 + c, :] for c in range(3)]
-        sent = [CX.at[:, 4:5, :], BX.at[:, 4:5, :]]
-        sent += [XR.at[:, :, c : c + 1, :] for c in range(3)]
-        remotes = [
-            pltpu.make_async_remote_copy(
-                src_ref=sources[i],
-                dst_ref=sent[i],
-                send_sem=far_send.at[i],
-                recv_sem=far_recv.at[i],
-                device_id=to_far,
-                device_id_type=pl.DeviceIdType.MESH,
-            )
-            for i in range(5)
-        ]
-        locals_ = [pltpu.make_async_copy(sources[i], kept[i], far_local.at[i]) for i in range(5)]
-        return remotes, locals_
-
-    @pl.when(is_far)
-    def _():
-        pl.semaphore_wait(barrier, count)
-
-    for side in range(2):
-
-        @pl.when(far[side])
-        def _():
-            remotes, locals_ = far_moves(side)
-            for copy in remotes + locals_:
-                copy.start()
-
-    for piece in range(PIECES):
-        send_halo(0, piece, is_far)
+        return (C.at[:, edge, :], B.at[:, edge, :])[i] if i < 2 else U.at[:, :, i - 2, edge, :]
+
+    def far_target(i, first):
+        at = pl.ds(first if i < 2 else first + i - 2, 1)
+        return (CX.at[:, at, :], BX.at[:, at, :])[i] if i < 2 else XR.at[:, :, at, :]
+
+    def far_copy(side, i):
+        return pltpu.make_async_remote_copy(
+            src_ref=far_source(side, i),
+            dst_ref=far_target(i, 4 if i < 2 else 0),
+            send_sem=far_send.at[i],
+            recv_sem=far_recv.at[i],
+            device_id={"xy": ix + 1 if side else ix - 1},
+            device_id_type=pl.DeviceIdType.MESH,
+        )
+
+    def kept_copy(side, i):
+        return pltpu.make_async_copy(
+            far_source(side, i), far_target(i, 0 if i < 2 else 4), far_local.at[i]
+        )
+
+    def far_begin():
+        pl.semaphore_wait(barrier, 1)
+        for side in range(2):
+
+            @pl.when(far[side])
+            def _():
+                for i in range(5):
+                    far_copy(side, i).start()
+                for i in range(5):
+                    kept_copy(side, i).start()
+
+    def near_lam(side):
+        pl.when(place[side] < 2)(functools.partial(pass_lam, side))
+
+    def far_lam(side):
+        pl.when(place[side] == 2)(functools.partial(pass_lam, side))
+
+    def last_lam(side):
+        pl.when(place[side] >= 3)(functools.partial(pass_lam, side))
 
     near_side(send_info)
     far_side(send_info)
@@ -723,10 +756,9 @@
 
             @pl.when(far[side])
             def _():
-                remotes, locals_ = far_moves(side)
                 for i in range(2):
-                    locals_[i].wait()
-                    remotes[i].wait_recv()
+                    kept_copy(side, i).wait()
+                    far_copy(side, i).wait_recv()
 
         own = row < 4
 
@@ -781,9 +813,8 @@
 
             @pl.when(far[side])
             def _():
-                remotes, locals_ = far_moves(side)
                 for i in range(2, 5):
-                    remotes[i].wait_recv()
+                    far_copy(side, i).wait_recv()
 
         turned_by = [(d, FC[i]) for i, d in enumerate((-2, -1, 0, 1, 2))]
 
@@ -871,16 +902,22 @@
     for sweep in range(SWEEPS):
         sums = loop(0, depth, inner, (none, none), 4)
         if sweep == 0:
-            near_side(pass_lam)
+            near_side(near_lam)
         halves = [(none, none), (none, none)]
         for piece in range(PIECES):
             for side in range(2):
 
-                @pl.when(has["xy", side] if sweep else beside[side])
-                def _():
-                    halo_copy(sweep, side, piece).wait_recv()
+                if sweep == 0 and piece == 0:
+
+                    @pl.when(beside[side])
+                    def _():
+                        rows_moved(side).wait_recv()
 
                 if sweep:
+
+                    @pl.when(has["xy", side])
+                    def _():
+                        halo_copy(sweep, side, piece).wait_recv()
 
                     @pl.when(far[side])
                     def _():
@@ -904,6 +941,9 @@
         put(ends, sums[1], 1)
 
         near_side(functools.partial(own_sum, sweep))
+        if sweep == 0:
+            pl.when(is_far)(far_begin)
+            far_side(far_lam)
         far_side(functools.partial(own_sum, sweep))
         near_side(functools.partial(pass_chain, sweep))
 
@@ -933,7 +973,7 @@
         loop(0, depth, forward, none, 4)
         loop(0, depth, backward, none, 4)
         if sweep == 0:
-            far_side(pass_lam)
+            far_side(last_lam)
             for side in range(2):
                 lam = get(coef, 10 + side)
                 away = tuple(
@@ -999,11 +1039,14 @@
 
                 @pl.when(far[side])
                 def _():
-                    remotes, locals_ = far_moves(side)
-                    for copy in remotes:
-                        copy.wait_send()
-                    for copy in locals_[2:]:
-                        copy.wait()
+                    for i in range(5):
+                        far_copy(side, i).wait_send()
+                    for i in range(2, 5):
+                        kept_copy(side, i).wait()
+
+                @pl.when(beside[1 - side])
+                def _():
+                    rows_moved(side).wait_send()
 
         loop(0, depth, join, 0, 4)
 
@@ -1022,10 +1065,10 @@
             to_all(stage, lambda copy: copy.wait_send())
 
     for side in range(2):
-        for sweep in range(SWEEPS):
-
-            @pl.when(has["xy", 1 - side] if sweep else beside[1 - side])
-            def _():
+
+        @pl.when(has["xy", 1 - side])
+        def _():
+            for sweep in range(1, SWEEPS):
                 for piece in range(PIECES):
                     halo_copy(sweep, side, piece).wait_send()
 
@@ -1033,26 +1076,28 @@
 
         @pl.when(sends)
         def _():
-            for j in range(3):
-                info_copy(side, j).wait_send()
+            chain_copy(
+                info_out.at[side, 0:3],
+                info_in.at[side, 0:3],
+                tip_send.at[side],
+                info_recv.at[side],
+                side,
+                1,
+            ).wait_send()
+            for sweep in range(SWEEPS):
+                own_copy(sweep, side, whole).wait_send()
+
+        @pl.when(both(sends, place[side] > 0))
+        def _():
+            info_copy(side).wait_send()
+
+        for steps in (2, 1):
+
+            @pl.when(both(odd[side], onward[side] >= steps))
+            def _():
+                lam_copy(side, steps, whole).wait_send()
                 for sweep in range(SWEEPS):
-                    own_copy(sweep, side, j).wait_send()
-
-        @pl.when(both(sends, place[side] > 0))
-        def _():
-            for j in range(3, 9):
-                info_copy(side, j).wait_send()
-            for j in range(3):
-                extra_copy(side, j).wait_send()
-
-        for steps in (2, 1):
-
-            @pl.when(both(odd[side], onward[side] >= steps))
-            def _():
-                for j in range(3):
-                    lam_copy(side, steps, j).wait_send()
-                    for sweep in range(SWEEPS):
-                        x_copy(sweep, side, steps, j).wait_send()
+                    x_copy(sweep, side, steps, whole).wait_send()
 
 
 def local(ngz, nxy, field, source, classes, boundary, conductance, angles, strengths):
@@ -1098,8 +1143,6 @@
             pltpu.VMEM((2, 9) + pair, f32),
             pltpu.VMEM((2, 3) + pair, f32),
             pltpu.VMEM((2, 3) + pair, f32),
-            pltpu.VMEM((2, 3) + pair, f32),
-            pltpu.VMEM((2, 3) + pair, f32),
             pltpu.VMEM((SWEEPS, 2, 3) + pair, f32),
             pltpu.VMEM((SWEEPS, 2, 3) + pair, f32),
             pltpu.VMEM((SWEEPS, 2, 3) + pair, f32),
@@ -1116,21 +1159,24 @@
             pltpu.VMEM((6, 10, rows, width), f32),
             pltpu.VMEM((10, rows, width), f32),
             dma((PIECES + 3,)),
-            dma((SWEEPS, 2, PIECES)),
-            dma((SWEEPS, 2, PIECES)),
-            dma((2, 9)),
-            dma((2, 9)),
-            dma((2, 2, 3)),
+            dma((2, PIECES)),
+            dma((2, PIECES)),
+            dma((2,)),
             dma((2, 3)),
+            dma((2,)),
+            dma((2,)),
+            dma((2, 2)),
             dma((2, 3)),
-            dma((2, 3)),
+            dma((SWEEPS, 2)),
             dma((SWEEPS, 2, 3)),
-            dma((SWEEPS, 2, 3)),
-            dma((SWEEPS, 2, 2, 3)),
+            dma((SWEEPS, 2, 2)),
             dma((SWEEPS, 2, 3)),
             dma((5,)),
             dma((5,)),
             dma((5,)),
+            pltpu.SemaphoreType.REGULAR,
+            dma((2,)),
+            dma((2,)),
             dma((6, 2)),
             dma((6, 2)),
         ],

time: 35.9 us -> 33.2 us (0.925)
  Pallas kernels: 34.9 us -> 32.2 us
    pallas_call x1, Pallas kernels: 34.9 us -> 32.2 us  [local(): pl.pallas_call(functools.partial(relax, ngz, nxy), out_shape=pltpu.VMEM(f...]
where the time goes in v2:
time: 33.2 us; the launch traced here: 33.1 us
  Pallas kernels  32.2 us (97%)
  local copies, waits for them, and re-layouts  0.88 us (3%)
    pallas_call x1, Pallas kernels, local(): pl.pallas_call(functools.partial(relax, ngz, nxy), out_shape=pltpu.VMEM(f...  32.2 us
    unnamed x1, local copies, waits for them, and re-layouts  0.88 us

profile of v2, /device:TPU:160, one launch (start us, length us, event | category | flops | bytes accessed | tf_op | source)
XLA Modules:
  0.0 33.1 jit_solution(7231083344809887)
XLA Ops:
  0.0 32.2 %shard_map.73 = f32[16,2,3,8,256]{4,3,2,1,0:T(8,128)S(1)} custom-call(f32[16,2,3,8,256]{4,3,2,1,0:T(8,128)} %field.1, f32[16,2,3,8,256]{4,3,2,1,0:T(8,128)} %source.1, s32[16,8,256]{2,1,0:T(8,128)} %classes.1, s32[16,8,256]{2,1,0:T(8,128)} %boundary.1, f32[16]{0:T(128)} %conductance.1, f32[3]{0:T(128)} %angles.1, f32[3]{0:T(128)} %strengths.1), custom_call_target="tpu_custom_call" | custom-call | tf_op jit(solution)/shard_map/pallas_call | solution.py:1115
  32.2 0.9 %copy.9 = f32[16,2,3,8,256]{4,3,2,1,0:T(8,128)} copy(f32[16,2,3,8,256]{4,3,2,1,0:T(8,128)S(1)} %shard_map.73) | data formatting | bytes 1572864

commit v3 on v2

--- a/solution.py
+++ b/solution.py
@@ -101,6 +101,7 @@
     ch_in,
     ch_out,
     XR,
+    FA,
     CX,
     BX,
     FP,
@@ -130,6 +131,8 @@
     near_ready,
     row_send,
     row_recv,
+    early_send,
+    early_recv,
     mi_send,
     mi_recv,
 ):
@@ -227,9 +230,27 @@
     def send_halo(sweep, piece):
         for side in range(2):
 
-            @pl.when(has["xy", 1 - side])
+            @pl.when(beside[1 - side])
             def _():
                 halo_copy(sweep, side, piece).start()
+
+    def early_copy(side, p, c):
+        return remote(
+            halo_out.at[1, 1 - side, p, c],
+            FA.at[:, p, c, :],
+            early_send,
+            early_recv,
+            ("xy", side),
+        )
+
+    def early_moved(side):
+        return remote(
+            halo_out.at[1, 1 - side],
+            halo_out.at[1, 1 - side],
+            early_send,
+            early_recv,
+            ("xy", side),
+        )
 
     def row_copy(side, p, c):
         return remote(
@@ -259,7 +280,7 @@
 
         for sweep in range(SWEEPS):
 
-            @pl.when(jnp.logical_not(has["xy", side] if sweep else beside[side]))
+            @pl.when(jnp.logical_not(beside[side]))
             def _():
                 halo_in[sweep, side] = jnp.zeros(halo_in.shape[2:], jnp.float32)
 
@@ -571,7 +592,7 @@
 
     def far_target(i, first):
         at = pl.ds(first if i < 2 else first + i - 2, 1)
-        return (CX.at[:, at, :], BX.at[:, at, :])[i] if i < 2 else XR.at[:, :, at, :]
+        return (CX.at[0, :, at, :], BX.at[0, :, at, :])[i] if i < 2 else XR.at[:, :, at, :]
 
     def far_copy(side, i):
         return pltpu.make_async_remote_copy(
@@ -588,6 +609,14 @@
             far_source(side, i), far_target(i, 0 if i < 2 else 4), far_local.at[i]
         )
 
+    def line_copy(side, i):
+        first = rows - 1 if side else 0
+        edge = pl.ds(first if i < 2 else (first - 1 if side else first + 1), 1)
+        at = pl.ds(0 if i < 2 else 4, 1)
+        return pltpu.make_async_copy(
+            (C, B)[i % 2].at[:, edge, :], (CX, BX)[i % 2].at[1, :, at, :], far_local.at[5 + i]
+        )
+
     def far_begin():
         pl.semaphore_wait(barrier, 1)
         for side in range(2):
@@ -598,6 +627,8 @@
                     far_copy(side, i).start()
                 for i in range(5):
                     kept_copy(side, i).start()
+                for i in range(4):
+                    line_copy(side, i).start()
 
     def near_lam(side):
         pl.when(place[side] < 2)(functools.partial(pass_lam, side))
@@ -681,41 +712,31 @@
     part = lambda k: third == k
     used = third < 3
 
-    def mi_copy(steps, stage):
+    def mi_copy(k, steps, parts=slice(None)):
         slot = steps + 3 if steps < 0 else steps + 2
-        parts = pl.ds(0, 6) if stage == 0 else pl.ds(6, 4)
         return pltpu.make_async_remote_copy(
-            src_ref=mi_out.at[parts],
-            dst_ref=mi_in.at[5 - slot, parts],
-            send_sem=mi_send.at[slot, stage],
-            recv_sem=mi_recv.at[5 - slot, stage],
+            src_ref=mi_out.at[k, parts],
+            dst_ref=mi_in.at[k, 5 - slot, parts],
+            send_sem=mi_send.at[k, slot],
+            recv_sem=mi_recv.at[k, 5 - slot],
             device_id={"gz": iz + steps},
             device_id_type=pl.DeviceIdType.MESH,
         )
 
     all_steps = (-3, -2, -1, 1, 2, 3)
 
-    def to_all(stage, act):
+    def for_all(act):
         for steps in all_steps:
 
             @pl.when((iz + steps >= 0) & (iz + steps < ngz))
             def _():
-                act(mi_copy(steps, stage))
-
-    def from_all(stage):
-        for steps in all_steps:
-            slot = steps + 3 if steps < 0 else steps + 2
-
-            @pl.when((iz + steps >= 0) & (iz + steps < ngz))
-            def _():
-                pltpu.make_async_remote_copy(
-                    src_ref=mi_out.at[pl.ds(0, 6) if stage == 0 else pl.ds(6, 4)],
-                    dst_ref=mi_in.at[slot, pl.ds(0, 6) if stage == 0 else pl.ds(6, 4)],
-                    send_sem=mi_send.at[slot, stage],
-                    recv_sem=mi_recv.at[slot, stage],
-                    device_id={"gz": iz + steps},
-                    device_id_type=pl.DeviceIdType.MESH,
-                ).wait_recv()
+                act(steps)
+
+    def to_all(k, parts):
+        for_all(lambda steps: mi_copy(k, steps, parts).start())
+
+    def from_all(k):
+        for_all(lambda steps: mi_copy(k, -steps).wait_recv())
 
     def shifts(of):
         planes = []
@@ -739,7 +760,8 @@
 
             @pl.when(jnp.logical_not((iz + steps >= 0) & (iz + steps < ngz)))
             def _():
-                mi_in[slot] = jnp.zeros(mi_in.shape[1:], jnp.float32)
+                for k in range(2):
+                    mi_in[k, slot] = jnp.zeros(mi_in.shape[2:], jnp.float32)
 
         q = matrix()
         for i, (_, plane_) in enumerate(shifts(lambda j, k: q[k][j])):
@@ -751,19 +773,23 @@
             strength = jnp.where(part(j), strengths[j], strength)
         FC[10] = strength
 
-    def far_first():
+    own = row < 4
+
+    def far_first(k):
         for side in range(2):
 
             @pl.when(far[side])
             def _():
-                for i in range(2):
-                    kept_copy(side, i).wait()
-                    far_copy(side, i).wait_recv()
-
-        own = row < 4
+                if k == 0:
+                    for i in range(2):
+                        kept_copy(side, i).wait()
+                        far_copy(side, i).wait_recv()
+                else:
+                    for i in range(4):
+                        line_copy(side, i).wait()
 
         def far_diagonal(z, carry):
-            ids_tile, bound = CX[z], BX[z]
+            ids_tile, bound = CX[k, z], BX[k, z]
             ids = jnp.where(
                 own,
                 jnp.broadcast_to(ids_tile[0:1, :], plane),
@@ -775,81 +801,84 @@
             sigma = jnp.zeros(plane, jnp.float32)
             for kind in range(kinds):
                 sigma = jnp.where(ids == kind, conductance[kind], sigma)
-            FT[z, 0] = 2.0 + 4.0 * coupling + penalty * edge.astype(jnp.float32)
-            FT[z, 1] = sigma * FC[10]
+            FT[k, z, 0] = 2.0 + 4.0 * coupling + penalty * edge.astype(jnp.float32)
+            FT[k, z, 1] = sigma * FC[10]
             return carry
 
         loop(0, depth, far_diagonal, 0, 4)
 
-        def far_pivots(k, carry):
+        def far_pivots(z, carry):
             p, q = carry
-            d, f = get(FT, k), get(FT, depth - 1 - k)
+            d, f = get(FT, k, z), get(FT, k, depth - 1 - z)
             p = inv((d[0] - p[0], d[1] - p[1]))
             q = inv((f[0] - q[0], f[1] - q[1]))
-            put(FP, p, k)
-            put(FPHI, q, depth - 1 - k)
+            put(FP, p, k, z)
+            put(FPHI, q, k, depth - 1 - z)
             return p, q
 
         loop(0, depth, far_pivots, ((zero, zero), (zero, zero)), 2)
         one = jnp.ones(plane, jnp.float32)
 
-        def far_columns(k, carry):
+        def far_columns(z, carry):
             down, up = carry
-            back = depth - 1 - k
-            down = mul(get(FPHI, k), down)
-            up = mul(get(FP, back), up)
-            put(FPHI, down, k)
-            put(FPSI, up, back)
+            back = depth - 1 - z
+            down = mul(get(FPHI, k, z), down)
+            up = mul(get(FP, k, back), up)
+            put(FPHI, down, k, z)
+            put(FPSI, up, k, back)
             return down, up
 
         loop(0, depth, far_columns, ((one, zero), (one, zero)), 2)
-        for i, value in enumerate((get(FPHI, 0), get(FPSI, depth - 1), get(FPSI, 0))):
-            mi_out[2 * i] = value[0]
-            mi_out[2 * i + 1] = value[1]
-        to_all(0, lambda copy: copy.start())
-
-    def far_second():
-        for side in range(2):
-
-            @pl.when(far[side])
-            def _():
-                for i in range(2, 5):
-                    far_copy(side, i).wait_recv()
-
+        ends_ = (get(FPHI, k, 0), get(FPSI, k, depth - 1), get(FPSI, k, 0))
+        for i, value in enumerate(ends_):
+            mi_out[k, 2 * i] = value[0]
+            mi_out[k, 2 * i + 1] = value[1]
+        to_all(k, pl.ds(0, 6))
+
+    def far_solve(k, rhs):
         turned_by = [(d, FC[i]) for i, d in enumerate((-2, -1, 0, 1, 2))]
 
         def far_sums(z, carry):
             first, last = carry
             t = tuple(
-                mix(turned_by, jnp.where(used, coupling * XR[z, p], zero)) for p in range(2)
+                mix(turned_by, jnp.where(used, coupling * rhs(z, p), zero)) for p in range(2)
             )
-            put(FT, t, z)
-            return add(first, mul(get(FPHI, z), t)), add(last, mul(get(FPSI, z), t))
+            put(FT, t, k, z)
+            return add(first, mul(get(FPHI, k, z), t)), add(last, mul(get(FPSI, k, z), t))
 
         first, last = loop(0, depth, far_sums, ((zero, zero), (zero, zero)), 4)
         for i, value in enumerate((first, last)):
-            mi_out[6 + 2 * i] = value[0]
-            mi_out[7 + 2 * i] = value[1]
-        to_all(1, lambda copy: copy.start())
+            mi_out[k, 6 + 2 * i] = value[0]
+            mi_out[k, 7 + 2 * i] = value[1]
+        to_all(k, pl.ds(6, 4))
 
         def far_forward(z, m):
-            m = mul(get(FP, z), add(get(FT, z), m))
-            put(FT, m, z)
+            m = mul(get(FP, k, z), add(get(FT, k, z), m))
+            put(FT, m, k, z)
             return m
 
-        def far_backward(k, w):
-            z = depth - 1 - k
-            w = add(get(FT, z), mul(get(FP, z), w))
-            put(FT, w, z)
+        def far_backward(i, w):
+            z = depth - 1 - i
+            w = add(get(FT, k, z), mul(get(FP, k, z), w))
+            put(FT, w, k, z)
             return w
 
         loop(0, depth, far_forward, (zero, zero), 4)
         loop(0, depth, far_backward, (zero, zero), 4)
 
-    def far_third():
-        from_all(0)
-        from_all(1)
-        block = lambda slot: [(mi_in[slot, 2 * i], mi_in[slot, 2 * i + 1]) for i in range(5)]
+    def far_second():
+        for side in range(2):
+
+            @pl.when(far[side])
+            def _():
+                for i in range(2, 5):
+                    far_copy(side, i).wait_recv()
+
+        far_solve(0, lambda z, p: XR[z, p])
+
+    def far_meet(k, take):
+        from_all(k)
+        block = lambda slot: [(mi_in[k, slot, 2 * i], mi_in[k, slot, 2 * i + 1]) for i in range(5)]
         x = lam = y = mu = (zero, zero)
         for slot in range(3):
             top, bottom, cross, first, last = block(slot)
@@ -865,38 +894,61 @@
                 add(first, mul(cross, mul(det, add(y, mul(mu, last))))),
                 add(top, mul(mul(cross, cross), mul(det, mu))),
             )
-        top, bottom, cross, first, last = [(mi_out[2 * i], mi_out[2 * i + 1]) for i in range(5)]
+        top, bottom, cross, first, last = [(mi_out[k, 2 * i], mi_out[k, 2 * i + 1]) for i in range(5)]
         g, h = add(x, mul(lam, first)), add(y, mul(mu, last))
         alpha, beta = one_minus(mul(lam, top)), one_minus(mul(mu, bottom))
         lc, mc = mul(lam, cross), mul(mu, cross)
         both_ = mul(lc, mc)
-        whole = mul(alpha, beta)
-        det = inv((whole[0] - both_[0], whole[1] - both_[1]))
+        all_ = mul(alpha, beta)
+        det = inv((all_[0] - both_[0], all_[1] - both_[1]))
         put(far_ends, mul(det, add(mul(g, beta), mul(lc, h))), 0)
         put(far_ends, mul(det, add(mul(h, alpha), mul(mc, g))), 1)
         back_by = [(d, FC[5 + i]) for i, d in enumerate((-2, -1, 0, 1, 2))]
-        here = row == jnp.where(far[1], rows - 1, 0)
 
         def far_join(z, carry):
             before, after = get(far_ends, 0), get(far_ends, 1)
-            w = add(add(get(FT, z), mul(get(FPHI, z), before)), mul(get(FPSI, z), after))
+            w = add(
+                add(get(FT, k, z), mul(get(FPHI, k, z), before)), mul(get(FPSI, k, z), after)
+            )
             for p in range(2):
-                u = mix(back_by, w[p])
-                FT[z, p] = u
-                for c in range(3):
-                    U[z, p, c] += jnp.where(here, jnp.broadcast_to(u[c : c + 1, :], plane), zero)
+                take(z, p, mix(back_by, w[p]))
             return carry
 
         loop(0, depth, far_join, 0, 4)
 
-    def add_far_row(side, piece):
-        def one_row(z, carry):
-            for p in range(2):
-                for c in range(3):
-                    halo_in[1, side, p, c, pl.ds(z, 1), :] += FT[z, p, 4 + c : 5 + c, :]
-            return carry
-
-        loop(piece * zs, (piece + 1) * zs, one_row, 0, 4)
+    def far_third():
+        def keep(z, p, u):
+            FT[0, z, p] = u
+
+        far_meet(0, keep)
+        for side in range(2):
+
+            @pl.when(far[side])
+            def _():
+                early_moved(side).wait_recv()
+
+        def rhs(z, p):
+            u = FT[0, z, p]
+            beside_ = jnp.where(lane == 0, zero, pltpu.roll(u, 1, 1))
+            beside_ += jnp.where(lane == width - 1, zero, pltpu.roll(u, width - 1, 1))
+            early = jnp.where(row < 3, FA[z, p], zero)
+            return pltpu.roll(u, 4, 0) + jnp.where(own, beside_ + early, zero)
+
+        far_solve(1, rhs)
+
+    def far_last():
+        here = row == jnp.where(far[1], rows - 1, 0)
+        next_ = row == jnp.where(far[1], rows - 2, 1)
+
+        def give(z, p, u):
+            for c in range(3):
+                OUT[z, p, c] += jnp.where(
+                    here,
+                    jnp.broadcast_to(u[c : c + 1, :], plane),
+                    jnp.where(next_, jnp.broadcast_to(u[4 + c : 5 + c, :], plane), zero),
+                )
+
+        far_meet(1, give)
 
     loads[PIECES + 2].wait()
     for sweep in range(SWEEPS):
@@ -915,13 +967,9 @@
 
                 if sweep:
 
-                    @pl.when(has["xy", side])
+                    @pl.when(beside[side])
                     def _():
                         halo_copy(sweep, side, piece).wait_recv()
-
-                    @pl.when(far[side])
-                    def _():
-                        add_far_row(side, piece)
 
                 for tile in tiles[piece * len(tiles) // PIECES : (piece + 1) * len(tiles) // PIECES]:
                     halves[side] = outer(sweep, side, tile, halves[side])
@@ -972,6 +1020,8 @@
 
         loop(0, depth, forward, none, 4)
         loop(0, depth, backward, none, 4)
+        if sweep:
+            pl.when(is_far)(far_third)
         if sweep == 0:
             far_side(last_lam)
             for side in range(2):
@@ -1019,6 +1069,13 @@
                     for side in range(2):
                         join_edge(side, tile)
                 send_halo(sweep + 1, piece)
+            for side in range(2):
+
+                @pl.when(far[side])
+                def _():
+                    for p in range(2):
+                        for c in range(3):
+                            early_copy(side, p, c).start()
 
 
         def join(z, carry):
@@ -1055,22 +1112,29 @@
             @pl.when(is_far)
             def _():
                 far_setup()
-                far_first()
+                far_first(0)
                 far_second()
-                far_third()
+                far_first(1)
+
+        else:
+            pl.when(is_far)(far_last)
 
     @pl.when(is_far)
     def _():
-        for stage in range(2):
-            to_all(stage, lambda copy: copy.wait_send())
+        for k in range(2):
+            for_all(lambda steps: mi_copy(k, steps).wait_send())
 
     for side in range(2):
 
-        @pl.when(has["xy", 1 - side])
+        @pl.when(beside[1 - side])
         def _():
             for sweep in range(1, SWEEPS):
                 for piece in range(PIECES):
                     halo_copy(sweep, side, piece).wait_send()
+
+        @pl.when(far[side])
+        def _():
+            early_moved(side).wait_send()
 
         sends = both(even[side], onward[side] >= 1)
 
@@ -1109,6 +1173,7 @@
     pair = (2, rows, width)
     edge = (2, 2, 3, depth, width)
     narrow = pltpu.VMEM((depth, 2, rows, width), f32)
+    lines = pltpu.VMEM((2, depth, 2, rows, width), f32)
     dma = pltpu.SemaphoreType.DMA
     hbm = pl.BlockSpec(memory_space=pl.ANY)
     smem = pl.BlockSpec(memory_space=pltpu.SMEM)
@@ -1148,16 +1213,17 @@
             pltpu.VMEM((SWEEPS, 2, 3) + pair, f32),
             pltpu.VMEM((SWEEPS, 2, 3) + pair, f32),
             narrow,
-            pltpu.VMEM(flat, jnp.int32),
-            pltpu.VMEM(flat, jnp.int32),
             narrow,
-            narrow,
-            narrow,
-            narrow,
+            pltpu.VMEM((2,) + flat, jnp.int32),
+            pltpu.VMEM((2,) + flat, jnp.int32),
+            lines,
+            lines,
+            lines,
+            lines,
             pltpu.VMEM((11, rows, width), f32),
             pltpu.VMEM((2,) + pair, f32),
-            pltpu.VMEM((6, 10, rows, width), f32),
-            pltpu.VMEM((10, rows, width), f32),
+            pltpu.VMEM((2, 6, 10, rows, width), f32),
+            pltpu.VMEM((2, 10, rows, width), f32),
             dma((PIECES + 3,)),
             dma((2, PIECES)),
             dma((2, PIECES)),
@@ -1171,14 +1237,16 @@
             dma((SWEEPS, 2, 3)),
             dma((SWEEPS, 2, 2)),
             dma((SWEEPS, 2, 3)),
-            dma((5,)),
+            dma((9,)),
             dma((5,)),
             dma((5,)),
             pltpu.SemaphoreType.REGULAR,
             dma((2,)),
             dma((2,)),
-            dma((6, 2)),
-            dma((6, 2)),
+            dma(()),
+            dma(()),
+            dma((2, 6)),
+            dma((2, 6)),
         ],
         compiler_params=pltpu.CompilerParams(collective_id=0, has_side_effects=True, vmem_limit_bytes=VMEM_LIMIT),
     )(field, source, classes, boundary, conductance, angles, strengths)

time: 33.2 us -> 31.1 us (0.937)
  Pallas kernels: 32.2 us -> 30.1 us
    pallas_call x1, Pallas kernels: 32.2 us -> 30.1 us  [local(): pl.pallas_call(functools.partial(relax, ngz, nxy), out_shape=pltpu.VMEM(f...]
where the time goes in v3:
time: 31.1 us; the launch traced here: 30.9 us
  Pallas kernels  30.1 us (97%)
  local copies, waits for them, and re-layouts  0.88 us (3%)
    pallas_call x1, Pallas kernels, local(): pl.pallas_call(functools.partial(relax, ngz, nxy), out_shape=pltpu.VMEM(f...  30.1 us
    unnamed x1, local copies, waits for them, and re-layouts  0.88 us

profile of v3, /device:TPU:160, one launch (start us, length us, event | category | flops | bytes accessed | tf_op | source)
XLA Modules:
  0.0 30.9 jit_solution(6178646978647924723)
XLA Ops:
  0.0 30.1 %shard_map.73 = f32[16,2,3,8,256]{4,3,2,1,0:T(8,128)S(1)} custom-call(f32[16,2,3,8,256]{4,3,2,1,0:T(8,128)} %field.1, f32[16,2,3,8,256]{4,3,2,1,0:T(8,128)} %source.1, s32[16,8,256]{2,1,0:T(8,128)} %classes.1, s32[16,8,256]{2,1,0:T(8,128)} %boundary.1, f32[16]{0:T(128)} %conductance.1, f32[3]{0:T(128)} %angles.1, f32[3]{0:T(128)} %strengths.1), custom_call_target="tpu_custom_call" | custom-call | tf_op jit(solution)/shard_map/pallas_call | solution.py:1180
  30.1 0.9 %copy.9 = f32[16,2,3,8,256]{4,3,2,1,0:T(8,128)} copy(f32[16,2,3,8,256]{4,3,2,1,0:T(8,128)S(1)} %shard_map.73) | data formatting | bytes 1572864

commit v4 on v3

--- a/solution.py
+++ b/solution.py
@@ -385,12 +385,15 @@
             device_id_type=pl.DeviceIdType.MESH,
         )
 
+    whole = slice(None)
+    way = (lambda side: 0) if ngz == 4 else (lambda side: side)
+
     def tip_copy(side, j):
         return chain_copy(
             info_out.at[side, j],
             info_in.at[side, j],
-            tip_send.at[side],
-            tip_recv.at[side, j],
+            tip_send.at[way(side)],
+            tip_recv.at[way(side), j],
             side,
             1,
         )
@@ -399,8 +402,8 @@
         return chain_copy(
             info_out.at[side, 3:9],
             info_in.at[side, 3:9],
-            info_send.at[side],
-            info_recv.at[side],
+            info_send.at[way(side)],
+            info_recv.at[way(side)],
             side,
             1,
         )
@@ -409,8 +412,8 @@
         return chain_copy(
             lam_out.at[side, j],
             lam_in.at[side, j],
-            lam_send.at[side, steps - 1],
-            lam_recv.at[side, j],
+            lam_send.at[way(side), steps - 1],
+            lam_recv.at[way(side), j],
             side,
             steps,
         )
@@ -419,8 +422,8 @@
         return chain_copy(
             own_out.at[sweep, side, j],
             own_in.at[sweep, side, j],
-            own_send.at[sweep, side],
-            own_recv.at[sweep, side, j],
+            own_send.at[sweep, way(side)],
+            own_recv.at[sweep, way(side), j],
             side,
             1,
         )
@@ -429,13 +432,12 @@
         return chain_copy(
             ch_out.at[sweep, side, j],
             ch_in.at[sweep, side, j],
-            ch_send.at[sweep, side, steps - 1],
-            ch_recv.at[sweep, side, j],
+            ch_send.at[sweep, way(side), steps - 1],
+            ch_recv.at[sweep, way(side), j],
             side,
             steps,
         )
 
-    whole = slice(None)
 
     both = jnp.logical_and
 
@@ -598,23 +600,40 @@
         return pltpu.make_async_remote_copy(
             src_ref=far_source(side, i),
             dst_ref=far_target(i, 4 if i < 2 else 0),
-            send_sem=far_send.at[i],
-            recv_sem=far_recv.at[i],
+            send_sem=far_send.at[min(i, 2)],
+            recv_sem=far_recv.at[min(i, 2)],
             device_id={"xy": ix + 1 if side else ix - 1},
             device_id_type=pl.DeviceIdType.MESH,
         )
 
     def kept_copy(side, i):
         return pltpu.make_async_copy(
-            far_source(side, i), far_target(i, 0 if i < 2 else 4), far_local.at[i]
-        )
+            far_source(side, i), far_target(i, 0 if i < 2 else 4), far_local.at[min(i, 2)]
+        )
+
+    def field_moved(side):
+        return pltpu.make_async_remote_copy(
+            src_ref=XR.at[:, :, 0:3, :],
+            dst_ref=XR.at[:, :, 0:3, :],
+            send_sem=far_send.at[2],
+            recv_sem=far_recv.at[2],
+            device_id={"xy": ix + 1 if side else ix - 1},
+            device_id_type=pl.DeviceIdType.MESH,
+        )
+
+    def field_kept():
+        return pltpu.make_async_copy(XR.at[:, :, 4:7, :], XR.at[:, :, 4:7, :], far_local.at[2])
+
+    def lines_kept(i):
+        ref = (CX, BX)[i].at[1, :, 0:2, :]
+        return pltpu.make_async_copy(ref, ref, far_local.at[3 + i])
 
     def line_copy(side, i):
         first = rows - 1 if side else 0
         edge = pl.ds(first if i < 2 else (first - 1 if side else first + 1), 1)
         at = pl.ds(0 if i < 2 else 4, 1)
         return pltpu.make_async_copy(
-            (C, B)[i % 2].at[:, edge, :], (CX, BX)[i % 2].at[1, :, at, :], far_local.at[5 + i]
+            (C, B)[i % 2].at[:, edge, :], (CX, BX)[i % 2].at[1, :, at, :], far_local.at[3 + i % 2]
         )
 
     def far_begin():
@@ -712,31 +731,48 @@
     part = lambda k: third == k
     used = third < 3
 
-    def mi_copy(k, steps, parts=slice(None)):
+    def mi_copy(k, steps, parts):
         slot = steps + 3 if steps < 0 else steps + 2
         return pltpu.make_async_remote_copy(
             src_ref=mi_out.at[k, parts],
             dst_ref=mi_in.at[k, 5 - slot, parts],
-            send_sem=mi_send.at[k, slot],
-            recv_sem=mi_recv.at[k, 5 - slot],
+            send_sem=mi_send.at[slot],
+            recv_sem=mi_recv.at[0 if k == whole else k, 5 - slot],
             device_id={"gz": iz + steps},
             device_id_type=pl.DeviceIdType.MESH,
         )
 
     all_steps = (-3, -2, -1, 1, 2, 3)
-
-    def for_all(act):
+    at_end = lambda k: jnp.logical_or(k == 0, k == ngz - 1)
+
+    def for_all(of, act):
         for steps in all_steps:
-
-            @pl.when((iz + steps >= 0) & (iz + steps < ngz))
-            def _():
-                act(steps)
-
-    def to_all(k, parts):
-        for_all(lambda steps: mi_copy(k, steps, parts).start())
+            there = (iz + steps >= 0) & (iz + steps < ngz)
+            edge_ = at_end(iz + steps * of)
+
+            @pl.when(jnp.logical_and(there, edge_))
+            def _():
+                act(steps, True)
+
+            @pl.when(jnp.logical_and(there, jnp.logical_not(edge_)))
+            def _():
+                act(steps, False)
+
+    def to_all(k, first):
+        def act(steps, ends_only):
+            if not ends_only:
+                parts = pl.ds(first, 4 if first else 6)
+            else:
+                parts = pl.ds(first + (2 if steps > 0 else 0), 2)
+            mi_copy(k, steps, parts).start()
+
+        for_all(0, act)
+
+    def moved(ends_only):
+        return pl.ds(0, 4 if ends_only else 10)
 
     def from_all(k):
-        for_all(lambda steps: mi_copy(k, -steps).wait_recv())
+        for_all(1, lambda steps, e: mi_copy(k, -steps, moved(e)).wait_recv())
 
     def shifts(of):
         planes = []
@@ -755,14 +791,24 @@
             total = term if total is None else total + term
         return total
 
+    def far_clear():
+        none_ = jnp.zeros((2,) + plane, jnp.float32)
+        for slot, steps in enumerate(all_steps):
+            there = (iz + steps >= 0) & (iz + steps < ngz)
+
+            @pl.when(jnp.logical_not(there))
+            def _():
+                for k in range(2):
+                    for part_ in range(5):
+                        mi_in[k, slot, 2 * part_ : 2 * part_ + 2] = none_
+
+            @pl.when(jnp.logical_and(there, at_end(iz + steps)))
+            def _():
+                for k in range(2):
+                    for part_ in (0, 2, 3) if steps < 0 else (1, 2, 4):
+                        mi_in[k, slot, 2 * part_ : 2 * part_ + 2] = none_
+
     def far_setup():
-        for slot, steps in enumerate(all_steps):
-
-            @pl.when(jnp.logical_not((iz + steps >= 0) & (iz + steps < ngz)))
-            def _():
-                for k in range(2):
-                    mi_in[k, slot] = jnp.zeros(mi_in.shape[2:], jnp.float32)
-
         q = matrix()
         for i, (_, plane_) in enumerate(shifts(lambda j, k: q[k][j])):
             FC[i] = plane_
@@ -785,8 +831,8 @@
                         kept_copy(side, i).wait()
                         far_copy(side, i).wait_recv()
                 else:
-                    for i in range(4):
-                        line_copy(side, i).wait()
+                    for i in range(2):
+                        lines_kept(i).wait()
 
         def far_diagonal(z, carry):
             ids_tile, bound = CX[k, z], BX[k, z]
@@ -833,7 +879,9 @@
         for i, value in enumerate(ends_):
             mi_out[k, 2 * i] = value[0]
             mi_out[k, 2 * i + 1] = value[1]
-        to_all(k, pl.ds(0, 6))
+
+    def send_columns(k):
+        to_all(k, 0)
 
     def far_solve(k, rhs):
         turned_by = [(d, FC[i]) for i, d in enumerate((-2, -1, 0, 1, 2))]
@@ -850,7 +898,7 @@
         for i, value in enumerate((first, last)):
             mi_out[k, 6 + 2 * i] = value[0]
             mi_out[k, 7 + 2 * i] = value[1]
-        to_all(k, pl.ds(6, 4))
+        to_all(k, 6)
 
         def far_forward(z, m):
             m = mul(get(FP, k, z), add(get(FT, k, z), m))
@@ -871,8 +919,7 @@
 
             @pl.when(far[side])
             def _():
-                for i in range(2, 5):
-                    far_copy(side, i).wait_recv()
+                field_moved(side).wait_recv()
 
         far_solve(0, lambda z, p: XR[z, p])
 
@@ -993,6 +1040,13 @@
             pl.when(is_far)(far_begin)
             far_side(far_lam)
         far_side(functools.partial(own_sum, sweep))
+        if sweep:
+
+            @pl.when(is_far)
+            def _():
+                far_second()
+                send_columns(1)
+
         near_side(functools.partial(pass_chain, sweep))
 
         def forward(z, m):
@@ -1022,6 +1076,14 @@
         loop(0, depth, backward, none, 4)
         if sweep:
             pl.when(is_far)(far_third)
+        else:
+
+            @pl.when(is_far)
+            def _():
+                far_clear()
+                far_setup()
+                far_first(1)
+
         if sweep == 0:
             far_side(last_lam)
             for side in range(2):
@@ -1096,10 +1158,10 @@
 
                 @pl.when(far[side])
                 def _():
-                    for i in range(5):
+                    for i in range(2):
                         far_copy(side, i).wait_send()
-                    for i in range(2, 5):
-                        kept_copy(side, i).wait()
+                    field_moved(side).wait_send()
+                    field_kept().wait()
 
                 @pl.when(beside[1 - side])
                 def _():
@@ -1109,20 +1171,18 @@
 
         if not final:
 
+
             @pl.when(is_far)
             def _():
-                far_setup()
                 far_first(0)
-                far_second()
-                far_first(1)
+                send_columns(0)
 
         else:
             pl.when(is_far)(far_last)
 
     @pl.when(is_far)
     def _():
-        for k in range(2):
-            for_all(lambda steps: mi_copy(k, steps).wait_send())
+        for_all(0, lambda steps, e: mi_copy(whole, steps, moved(e)).wait_send())
 
     for side in range(2):
 
@@ -1143,8 +1203,8 @@
             chain_copy(
                 info_out.at[side, 0:3],
                 info_in.at[side, 0:3],
-                tip_send.at[side],
-                info_recv.at[side],
+                tip_send.at[way(side)],
+                info_recv.at[way(side)],
                 side,
                 1,
             ).wait_send()
@@ -1175,6 +1235,7 @@
     narrow = pltpu.VMEM((depth, 2, rows, width), f32)
     lines = pltpu.VMEM((2, depth, 2, rows, width), f32)
     dma = pltpu.SemaphoreType.DMA
+    ways = 1 if ngz == 4 else 2
     hbm = pl.BlockSpec(memory_space=pl.ANY)
     smem = pl.BlockSpec(memory_space=pltpu.SMEM)
     return pl.pallas_call(
@@ -1227,25 +1288,25 @@
             dma((PIECES + 3,)),
             dma((2, PIECES)),
             dma((2, PIECES)),
-            dma((2,)),
-            dma((2, 3)),
-            dma((2,)),
-            dma((2,)),
-            dma((2, 2)),
-            dma((2, 3)),
-            dma((SWEEPS, 2)),
-            dma((SWEEPS, 2, 3)),
-            dma((SWEEPS, 2, 2)),
-            dma((SWEEPS, 2, 3)),
-            dma((9,)),
+            dma((ways,)),
+            dma((ways, 3)),
+            dma((ways,)),
+            dma((ways,)),
+            dma((ways, 2)),
+            dma((ways, 3)),
+            dma((SWEEPS, ways)),
+            dma((SWEEPS, ways, 3)),
+            dma((SWEEPS, ways, 2)),
+            dma((SWEEPS, ways, 3)),
             dma((5,)),
-            dma((5,)),
+            dma((3,)),
+            dma((3,)),
             pltpu.SemaphoreType.REGULAR,
             dma((2,)),
             dma((2,)),
             dma(()),
             dma(()),
-            dma((2, 6)),
+            dma((6,)),
             dma((2, 6)),
         ],
         compiler_params=pltpu.CompilerParams(collective_id=0, has_side_effects=True, vmem_limit_bytes=VMEM_LIMIT),

time: 31.1 us -> 29.2 us (0.939); the launches traced: 30.9 us -> 28.7 us
  Pallas kernels: 30.1 us -> 27.8 us
    pallas_call x1, Pallas kernels: 30.1 us -> 27.8 us  [local(): pl.pallas_call(functools.partial(relax, ngz, nxy), out_shape=pltpu.VMEM(f...]
where the time goes in v4:
time: 29.2 us; the launch traced here: 28.7 us
  Pallas kernels  27.8 us (95%)
  local copies, waits for them, and re-layouts  0.88 us (3%)
    pallas_call x1, Pallas kernels, local(): pl.pallas_call(functools.partial(relax, ngz, nxy), out_shape=pltpu.VMEM(f...  27.8 us
    unnamed x1, local copies, waits for them, and re-layouts  0.88 us

profile of v4, /device:TPU:160, one launch (start us, length us, event | category | flops | bytes accessed | tf_op | source)
XLA Modules:
  0.0 28.7 jit_solution(14559779189337961384)
XLA Ops:
  0.0 27.8 %shard_map.73 = f32[16,2,3,8,256]{4,3,2,1,0:T(8,128)S(1)} custom-call(f32[16,2,3,8,256]{4,3,2,1,0:T(8,128)} %field.1, f32[16,2,3,8,256]{4,3,2,1,0:T(8,128)} %source.1, s32[16,8,256]{2,1,0:T(8,128)} %classes.1, s32[16,8,256]{2,1,0:T(8,128)} %boundary.1, f32[16]{0:T(128)} %conductance.1, f32[3]{0:T(128)} %angles.1, f32[3]{0:T(128)} %strengths.1), custom_call_target="tpu_custom_call" | custom-call | tf_op jit(solution)/shard_map/pallas_call | solution.py:1241
  27.8 0.9 %copy.9 = f32[16,2,3,8,256]{4,3,2,1,0:T(8,128)} copy(f32[16,2,3,8,256]{4,3,2,1,0:T(8,128)S(1)} %shard_map.73) | data formatting | bytes 1572864

commit v5 on v4

--- a/solution.py
+++ b/solution.py
@@ -1002,6 +1002,8 @@
         sums = loop(0, depth, inner, (none, none), 4)
         if sweep == 0:
             near_side(near_lam)
+        else:
+            pl.when(is_far)(far_second)
         halves = [(none, none), (none, none)]
         for piece in range(PIECES):
             for side in range(2):
@@ -1037,17 +1039,21 @@
 
         near_side(functools.partial(own_sum, sweep))
         if sweep == 0:
-            pl.when(is_far)(far_begin)
+
+            @pl.when(is_far)
+            def _():
+                far_begin()
+                near_side(functools.partial(pass_chain, sweep))
+
             far_side(far_lam)
         far_side(functools.partial(own_sum, sweep))
         if sweep:
-
-            @pl.when(is_far)
-            def _():
-                far_second()
-                send_columns(1)
-
-        near_side(functools.partial(pass_chain, sweep))
+            near_side(functools.partial(pass_chain, sweep))
+        else:
+
+            @pl.when(not_far)
+            def _():
+                near_side(functools.partial(pass_chain, sweep))
 
         def forward(z, m):
             given = []
@@ -1075,7 +1081,12 @@
         loop(0, depth, forward, none, 4)
         loop(0, depth, backward, none, 4)
         if sweep:
-            pl.when(is_far)(far_third)
+
+            @pl.when(is_far)
+            def _():
+                send_columns(1)
+                far_third()
+
         else:
 
             @pl.when(is_far)

time: 29.2 us -> 29.2 us (level)
  the two profiles are of different devices: /device:TPU:160 before, /device:TPU:31 now
where the time goes in v5:
time: 29.2 us; the launch traced here: 29.1 us
  Pallas kernels  28.2 us (97%)
  local copies, waits for them, and re-layouts  0.88 us (3%)
    pallas_call x1, Pallas kernels, local(): pl.pallas_call(functools.partial(relax, ngz, nxy), out_shape=pltpu.VMEM(f...  28.2 us
    unnamed x1, local copies, waits for them, and re-layouts  0.88 us

profile of v5, /device:TPU:31, one launch (start us, length us, event | category | flops | bytes accessed | tf_op | source)
XLA Modules:
  0.0 29.1 jit_solution(4420340140815741852)
XLA Ops:
  0.0 28.2 %shard_map.73 = f32[16,2,3,8,256]{4,3,2,1,0:T(8,128)S(1)} custom-call(f32[16,2,3,8,256]{4,3,2,1,0:T(8,128)} %field.1, f32[16,2,3,8,256]{4,3,2,1,0:T(8,128)} %source.1, s32[16,8,256]{2,1,0:T(8,128)} %classes.1, s32[16,8,256]{2,1,0:T(8,128)} %boundary.1, f32[16]{0:T(128)} %conductance.1, f32[3]{0:T(128)} %angles.1, f32[3]{0:T(128)} %strengths.1), custom_call_target="tpu_custom_call" | custom-call | tf_op jit(solution)/shard_map/pallas_call | solution.py:1252
  28.2 0.9 %copy.9 = f32[16,2,3,8,256]{4,3,2,1,0:T(8,128)} copy(f32[16,2,3,8,256]{4,3,2,1,0:T(8,128)S(1)} %shard_map.73) | data formatting | bytes 1572864

commit v6 on v4

--- a/solution.py
+++ b/solution.py
@@ -125,7 +125,6 @@
     own_recv,
     ch_send,
     ch_recv,
-    far_local,
     far_send,
     far_recv,
     near_ready,
@@ -222,7 +221,7 @@
         return remote(
             halo_out.at[sweep, side, :, :, span],
             halo_in.at[sweep, side, :, :, span],
-            halo_send.at[side, piece],
+            halo_send.at[side],
             halo_recv.at[side, piece],
             ("xy", 1 - side),
         )
@@ -608,7 +607,7 @@
 
     def kept_copy(side, i):
         return pltpu.make_async_copy(
-            far_source(side, i), far_target(i, 0 if i < 2 else 4), far_local.at[min(i, 2)]
+            far_source(side, i), far_target(i, 0 if i < 2 else 4), in_sems.at[min(i, 2)]
         )
 
     def field_moved(side):
@@ -622,18 +621,18 @@
         )
 
     def field_kept():
-        return pltpu.make_async_copy(XR.at[:, :, 4:7, :], XR.at[:, :, 4:7, :], far_local.at[2])
+        return pltpu.make_async_copy(XR.at[:, :, 4:7, :], XR.at[:, :, 4:7, :], in_sems.at[2])
 
     def lines_kept(i):
         ref = (CX, BX)[i].at[1, :, 0:2, :]
-        return pltpu.make_async_copy(ref, ref, far_local.at[3 + i])
+        return pltpu.make_async_copy(ref, ref, in_sems.at[3 + i])
 
     def line_copy(side, i):
         first = rows - 1 if side else 0
         edge = pl.ds(first if i < 2 else (first - 1 if side else first + 1), 1)
         at = pl.ds(0 if i < 2 else 4, 1)
         return pltpu.make_async_copy(
-            (C, B)[i % 2].at[:, edge, :], (CX, BX)[i % 2].at[1, :, at, :], far_local.at[3 + i % 2]
+            (C, B)[i % 2].at[:, edge, :], (CX, BX)[i % 2].at[1, :, at, :], in_sems.at[3 + i % 2]
         )
 
     def far_begin():
@@ -1045,7 +1044,6 @@
             @pl.when(is_far)
             def _():
                 far_second()
-                send_columns(1)
 
         near_side(functools.partial(pass_chain, sweep))
 
@@ -1075,7 +1073,12 @@
         loop(0, depth, forward, none, 4)
         loop(0, depth, backward, none, 4)
         if sweep:
-            pl.when(is_far)(far_third)
+
+            @pl.when(is_far)
+            def _():
+                send_columns(1)
+                far_third()
+
         else:
 
             @pl.when(is_far)
@@ -1188,9 +1191,13 @@
 
         @pl.when(beside[1 - side])
         def _():
-            for sweep in range(1, SWEEPS):
-                for piece in range(PIECES):
-                    halo_copy(sweep, side, piece).wait_send()
+            remote(
+                halo_out.at[1, side],
+                halo_in.at[1, side],
+                halo_send.at[side],
+                halo_recv.at[side, 0],
+                ("xy", 1 - side),
+            ).wait_send()
 
         @pl.when(far[side])
         def _():
@@ -1286,7 +1293,7 @@
             pltpu.VMEM((2, 6, 10, rows, width), f32),
             pltpu.VMEM((2, 10, rows, width), f32),
             dma((PIECES + 3,)),
-            dma((2, PIECES)),
+            dma((2,)),
             dma((2, PIECES)),
             dma((ways,)),
             dma((ways, 3)),
@@ -1298,7 +1305,6 @@
             dma((SWEEPS, ways, 3)),
             dma((SWEEPS, ways, 2)),
             dma((SWEEPS, ways, 3)),
-            dma((5,)),
             dma((3,)),
             dma((3,)),
             pltpu.SemaphoreType.REGULAR,

time: 29.2 us -> 29.1 us (level)
  no operation moved by 1% of the time
where the time goes in v6:
time: 29.1 us; the launch traced here: 28.6 us
  Pallas kernels  27.7 us (95%)
  local copies, waits for them, and re-layouts  0.88 us (3%)
    pallas_call x1, Pallas kernels, local(): pl.pallas_call(functools.partial(relax, ngz, nxy), out_shape=pltpu.VMEM(f...  27.7 us
    unnamed x1, local copies, waits for them, and re-layouts  0.88 us

profile of v6, /device:TPU:160, one launch (start us, length us, event | category | flops | bytes accessed | tf_op | source)
XLA Modules:
  0.0 28.6 jit_solution(1399305931568081161)
XLA Ops:
  0.0 27.7 %shard_map.73 = f32[16,2,3,8,256]{4,3,2,1,0:T(8,128)S(1)} custom-call(f32[16,2,3,8,256]{4,3,2,1,0:T(8,128)} %field.1, f32[16,2,3,8,256]{4,3,2,1,0:T(8,128)} %source.1, s32[16,8,256]{2,1,0:T(8,128)} %classes.1, s32[16,8,256]{2,1,0:T(8,128)} %boundary.1, f32[16]{0:T(128)} %conductance.1, f32[3]{0:T(128)} %angles.1, f32[3]{0:T(128)} %strengths.1), custom_call_target="tpu_custom_call" | custom-call | tf_op jit(solution)/shard_map/pallas_call | solution.py:1248
  27.7 0.9 %copy.9 = f32[16,2,3,8,256]{4,3,2,1,0:T(8,128)} copy(f32[16,2,3,8,256]{4,3,2,1,0:T(8,128)S(1)} %shard_map.73) | data formatting | bytes 1572864

commit v7 on v6

--- a/solution.py
+++ b/solution.py
@@ -693,19 +693,30 @@
             for p in range(2)
         ]
 
+    tall = lax.broadcasted_iota(jnp.int32, (rows, width // 2), 0)
+    slim = lax.broadcasted_iota(jnp.int32, (rows, width // 2), 1)
+
     def inner(z, carry):
         first, last = carry
         q = matrix()
+        half = width // 2
         driven = []
         for p in range(2):
             of = []
             for c in range(3):
-                u = U[z, p, c]
-                around = jnp.where(lane == 0, zero, pltpu.roll(u, 1, 1))
-                around += jnp.where(lane == width - 1, zero, pltpu.roll(u, width - 1, 1))
-                around += jnp.where(row == 0, zero, pltpu.roll(u, 1, 0))
-                around += jnp.where(row == rows - 1, zero, pltpu.roll(u, rows - 1, 0))
-                of.append(S[z, p, c] + coupling * around)
+                a, b = U[z, p, c, :, :half], U[z, p, c, :, half:]
+                al, bl = pltpu.roll(a, 1, 1), pltpu.roll(b, 1, 1)
+                ar, br = pltpu.roll(a, half - 1, 1), pltpu.roll(b, half - 1, 1)
+                low, high = slim == 0, slim == half - 1
+                around = []
+                for v, l, r in (
+                    (a, jnp.where(low, 0.0, al), jnp.where(high, br, ar)),
+                    (b, jnp.where(low, al, bl), jnp.where(high, 0.0, br)),
+                ):
+                    up = jnp.where(tall == 0, 0.0, pltpu.roll(v, 1, 0))
+                    down = jnp.where(tall == rows - 1, 0.0, pltpu.roll(v, rows - 1, 0))
+                    around.append((l + r) + (up + down))
+                of.append(S[z, p, c] + coupling * jnp.concatenate(around, axis=1))
             driven.append(of)
         turned = turn(q, driven)
         put(T, turned, z)

time: 29.1 us -> 29.9 us (1.027)
  Pallas kernels: 27.7 us -> 28.5 us
    pallas_call x1, Pallas kernels: 27.7 us -> 28.5 us  [local(): pl.pallas_call(functools.partial(relax, ngz, nxy), out_shape=pltpu.VMEM(f...]
where the time goes in v7:
time: 29.9 us; the launch traced here: 29.4 us
  Pallas kernels  28.5 us (95%)
  local copies, waits for them, and re-layouts  0.88 us (3%)
    pallas_call x1, Pallas kernels, local(): pl.pallas_call(functools.partial(relax, ngz, nxy), out_shape=pltpu.VMEM(f...  28.5 us
    unnamed x1, local copies, waits for them, and re-layouts  0.88 us

profile of v7, /device:TPU:160, one launch (start us, length us, event | category | flops | bytes accessed | tf_op | source)
XLA Modules:
  0.0 29.4 jit_solution(583797907649453496)
XLA Ops:
  0.0 28.5 %shard_map.73 = f32[16,2,3,8,256]{4,3,2,1,0:T(8,128)S(1)} custom-call(f32[16,2,3,8,256]{4,3,2,1,0:T(8,128)} %field.1, f32[16,2,3,8,256]{4,3,2,1,0:T(8,128)} %source.1, s32[16,8,256]{2,1,0:T(8,128)} %classes.1, s32[16,8,256]{2,1,0:T(8,128)} %boundary.1, f32[16]{0:T(128)} %conductance.1, f32[3]{0:T(128)} %angles.1, f32[3]{0:T(128)} %strengths.1), custom_call_target="tpu_custom_call" | custom-call | tf_op jit(solution)/shard_map/pallas_call | solution.py:1259
  28.5 0.9 %copy.9 = f32[16,2,3,8,256]{4,3,2,1,0:T(8,128)} copy(f32[16,2,3,8,256]{4,3,2,1,0:T(8,128)S(1)} %shard_map.73) | data formatting | bytes 1572864
